TPU v7x, 32 devices: a whole 2x2x4 slice. The times are simulated.
32 devices in a mesh: row: 4 (over y, x), col: 4 (over z), batch: 2 (over core).
Axes of the slice: x: 2, y: 2, z: 4, core: 2. Of those that a mesh axis runs over, the one named last changes fastest.
Arguments:
- item_ids: int32 [4, 4, 2048], P('batch', 'col', 'row'), parts along dimension 0, may hold values from 0 to 511
- pad_masks: int32 [4, 4, 2048], P('batch', 'col', 'row'), parts along dimension 0, may hold values from 0 to 1
- lengths: int32 [4], P('batch'), parts along dimension 0, may hold values from 7168 to 8192
- item_table: bfloat16 [512, 1024], replicated, may hold values from -5 to 5
- w_gate: bfloat16 [1024, 1024], replicated, may hold values from -0.1875 to 0.1875
- w_in: bfloat16 [1024, 1280], replicated, may hold values from -0.1875 to 0.1875
- w_dt: bfloat16 [1024, 8], replicated, may hold values from -0.1875 to 0.1875
- conv_taps: float32 [4, 1280], replicated, may hold values from -3 to 3
- dt_bias: float32 [8], replicated, may hold values from -2 to 1
- decay_rates: float32 [8], replicated, may hold values from 1.2207031e-05 to 0.05
- norm_gain: float32 [1024], replicated, may hold values from 0.1 to 1.9
- w_out: bfloat16 [1024, 1024], replicated, may hold values from -0.1875 to 0.1875
Outputs:
- result: bfloat16 [4, 4, 2048, 1024], P('batch', 'col', 'row'), parts along dimension 0
There are 2 independent parts, one for each index of `batch`. A program takes and returns all parts, laid end to end along the dimension named above; an argument that names none is the same for every part. Nothing has to cross between parts.
Inputs may be any that keep to these rules, and one draw needn't show every extreme that they name: `lengths`: every history keeps at least its first 7168 positions before padding.
All inputs are finite; a program needn't handle non-finite values.
Results may differ from a plain program's by a relative error of at most 0.0093.
Values may be sent and summed in bfloat16 or wider, within the bound.
A program may use at most 128 MiB of HBM per device.

v0:
```python
import jax
import jax.numpy as jnp
from jax import lax
from jax.sharding import PartitionSpec as P

STRETCH = 128


def passed_along(block, axis, distance):
    devices = range(lax.axis_size(axis))
    route = [((i - distance) % len(devices), i) for i in devices]
    return lax.ppermute(block, axis, route)


def from_behind(shard, axis, by):
    length = lax.axis_size(axis)
    pairs = [(i, i + by) for i in range(length) if 0 <= i + by < length]
    return lax.ppermute(shard, axis, pairs)


def carried_in(shard, axis, combine, identity):
    length, index = (lax.axis_size(axis), lax.axis_index(axis))
    everything = jax.tree.map(lambda part: lax.all_gather(part, axis), shard)
    start = jax.tree.map(
        lambda part, zero: jnp.broadcast_to(jnp.asarray(zero, part.dtype), part.shape),
        shard,
        identity,
    )

    def lap(k, before):
        reached = k < index
        new = combine(before, jax.tree.map(lambda part: part[k], everything))
        return jax.tree.map(lambda a, b: jnp.where(reached, a, b), new, before)

    return lax.fori_loop(0, length, lap, start)


def combine(earlier, later):
    return (earlier[0] + later[0], jnp.exp(-later[0])[..., None, None] * earlier[1] + later[1])


def choose_pair(condition, first_pair, second_pair):
    return (
        jnp.where(condition, first_pair[0], second_pair[0]),
        jnp.where(condition, first_pair[1], second_pair[1]),
    )


def per_device(
    item_ids,
    pad_masks,
    lengths,
    item_table,
    w_gate,
    w_in,
    w_dt,
    conv_taps,
    dt_bias,
    decay_rates,
    norm_gain,
    w_out,
):
    users = item_ids.shape[0]
    events = item_ids.shape[2]
    full_width = w_in.shape[1]
    inner_width = w_gate.shape[1]
    head_count = decay_rates.shape[0]
    head_size = inner_width // head_count
    state_width = (full_width - inner_width) // 2
    kernel = conv_taps.shape[0]
    row_count = lax.axis_size("row")
    row_place = lax.axis_index("row")
    col_place = lax.axis_index("col")
    stretch_count = events // STRETCH
    item_rows = item_ids[:, 0, :]
    embedded = jnp.take(item_table, item_rows, axis=0).reshape(users * events, -1)
    projected = (
        jnp.dot(embedded, w_in, preferred_element_type=jnp.float32)
        .astype(jnp.bfloat16)
        .reshape(users, events, full_width)
    )
    gate_rows = (
        jnp.dot(embedded, w_gate, preferred_element_type=jnp.float32)
        .astype(jnp.bfloat16)
        .reshape(users, events, inner_width)
    )
    step_raw = jnp.dot(embedded, w_dt, preferred_element_type=jnp.float32).reshape(
        users, events, head_count
    )
    at_start = jnp.logical_and(row_place == 0, col_place == 0)
    tail_rows = projected[:, events - (kernel - 1) :, :]
    from_row = passed_along(tail_rows, "row", 1)
    from_col = from_behind(from_row, "col", 1)
    before = jnp.where(row_place == 0, from_col, from_row)
    before = jnp.where(at_start, jnp.zeros_like(before), before)
    joined = jnp.concatenate([before, projected], axis=1)
    convolved = joined[:, 0:events, :].astype(jnp.float32) * conv_taps[0]
    for offset in range(1, kernel):
        convolved = (
            convolved
            + joined[:, offset : offset + events, :].astype(jnp.float32) * conv_taps[offset]
        )
    signal = jax.nn.silu(convolved[..., :inner_width]).astype(jnp.bfloat16)
    inward = convolved[..., inner_width : inner_width + state_width].astype(jnp.bfloat16)
    outward = convolved[..., inner_width + state_width :].astype(jnp.bfloat16)
    first_event = (col_place * row_count + row_place) * events
    position = first_event + lax.broadcasted_iota(jnp.int32, (users, events), 1)
    usable = jnp.logical_and(position < lengths[:, None], pad_masks[:, 0, :] > 0).astype(
        jnp.float32
    )
    step_size = usable[..., None] * jax.nn.softplus(step_raw + dt_bias)
    log_decay = jnp.cumsum(
        (step_size * decay_rates).reshape(users, stretch_count, STRETCH, head_count), axis=2
    )
    log_heads = jnp.moveaxis(log_decay, 3, 2)
    size_heads = jnp.moveaxis(step_size.reshape(users, stretch_count, STRETCH, head_count), 3, 2)
    signal_heads = signal.reshape(users, stretch_count, STRETCH, head_count, head_size)
    inward_stretches = inward.reshape(users, stretch_count, STRETCH, state_width)
    outward_stretches = outward.reshape(users, stretch_count, STRETCH, state_width)
    scores = jnp.einsum(
        "scqn,scun->scqu", outward_stretches, inward_stretches, preferred_element_type=jnp.float32
    )
    causal = lax.broadcasted_iota(jnp.int32, (STRETCH, STRETCH), 0) >= lax.broadcasted_iota(
        jnp.int32, (STRETCH, STRETCH), 1
    )
    log_gap = log_heads[..., :, None] - log_heads[..., None, :]
    decays = jnp.where(causal, jnp.exp(-jnp.where(causal, log_gap, 0.0)), 0.0)
    weights = (scores[:, :, None] * decays * size_heads[:, :, :, None, :]).astype(jnp.bfloat16)
    local_out = jnp.einsum(
        "schqu,scuhp->scqhp", weights, signal_heads, preferred_element_type=jnp.float32
    )
    tail_weight = jnp.exp(log_heads - log_heads[..., -1:]) * size_heads
    scaled_in = (inward_stretches[:, :, None] * tail_weight[..., None]).astype(jnp.bfloat16)
    stretch_states = jnp.einsum(
        "schun,scuhp->schpn", scaled_in, signal_heads, preferred_element_type=jnp.float32
    )
    stretch_logs = log_heads[..., -1]
    running = (
        jnp.zeros((users, head_count), jnp.float32),
        jnp.zeros((users, head_count, head_size, state_width), jnp.float32),
    )
    neutral = running
    inside = []
    for counter in range(stretch_count):
        inside.append(running)
        running = combine(running, (stretch_logs[:, counter], stretch_states[:, counter]))
    gathered = (
        lax.all_gather(running[0][None], "row", axis=0, tiled=True),
        lax.all_gather(running[1][None], "row", axis=0, tiled=True),
    )
    row_before = neutral
    block_sum = neutral
    for counter in range(row_count):
        member = (gathered[0][counter], gathered[1][counter])
        row_before = choose_pair(counter < row_place, combine(row_before, member), row_before)
        block_sum = combine(block_sum, member)
    block_before = carried_in(block_sum, "col", combine, neutral)
    col_state = block_before[1]
    carry_in = jnp.exp(-row_before[0])[..., None, None] * col_state + row_before[1]
    entering = jnp.stack(
        [jnp.exp(-pair[0])[..., None, None] * carry_in + pair[1] for pair in inside], axis=1
    ).astype(jnp.bfloat16)
    carried_out = (
        jnp.einsum(
            "scqn,schpn->scqhp", outward_stretches, entering, preferred_element_type=jnp.float32
        )
        * jnp.exp(-log_decay)[..., None]
    )
    mixture = (local_out + carried_out).reshape(users, events, inner_width)
    gated_rows = mixture * jax.nn.silu(gate_rows.astype(jnp.float32))
    normed = (
        gated_rows
        * lax.rsqrt(jnp.mean(gated_rows * gated_rows, axis=-1, keepdims=True) + 1.0)
        * norm_gain
    ).astype(jnp.bfloat16)
    result = jnp.dot(
        normed.reshape(users * events, inner_width), w_out, preferred_element_type=jnp.float32
    ).reshape(users, events, -1)
    result = result * usable[..., None]
    return result.astype(jnp.bfloat16)[:, None]


def solution(mesh):
    in_specs = (
        P("batch", "col", "row"),
        P("batch", "col", "row"),
        P("batch"),
        P(),
        P(),
        P(),
        P(),
        P(),
        P(),
        P(),
        P(),
        P(),
    )
    out_specs = P("batch", "col", "row", None)
    return jax.shard_map(
        per_device, mesh=mesh, in_specs=in_specs, out_specs=out_specs, check_vma=False
    )
```

profile of v0, /device:TPU:0, one launch (start us, length us, event | category | flops | bytes accessed | tf_op | source)
XLA Modules:
  0.0 226.2 jit_solution(9128841277364747442)
XLA Ops:
  8.1 7.4 %gather_fusion = bf16[1024,1024]{1,0:T(8,128)(2,1)} fusion(bf16[512,1024]{1,0:T(8,128)(2,1)} %param.17, s32[1024]{0:T(1024)S(1)} %broadcast_clamp_fusion), kind=kCustom, calls=%fused_computation | custom fusion | bytes 4198400 | tf_op jit(solution)/shard_map/jit(_take)/gather | solution.py:76
  15.5 4.6 %convolution_convert_fusion = bf16[1024,1280]{1,0:T(8,128)(2,1)S(1)} fusion(bf16[1024,1280]{1,0:T(8,128)(2,1)S(1)} %copy-done, bf16[1024,1024]{1,0:T(8,128)(2,1)} %gather_fusion, pred[1024]{0:T(1024)(128)(4,1)S(1)} %compare_and_fusion.1), kind=kOutput, calls=%fused_computation.21 | convolution fusion | flops 2686713856 | bytes 7341056 | tf_op jit(solution)/shard_map/dot_general | solution.py:78
  21.6 3.0 %collective-permute-start = (bf16[2,3,1280]{2,1,0:T(4,128)(2,1)S(1)}, bf16[2,3,1280]{2,1,0:T(4,128)(2,1)S(1)}, u32[]{:S(2)}, u32[]{:S(2)}) collective-permute-start(bf16[2,3,1280]{2,1,0:T(4,128)(2,1)S(1)} %slice.121), channel_id=1, source_target_pairs={{24,0},{0,8},{8,16},{16,24},{25,1},{1,9},{9,17},{17,25},{26,2},{2,... | collective-permute-start | bytes 46088 | tf_op jit(solution)/shard_map/ppermute | solution.py:12
  24.7 2.3 %fusion.46 = f32[2,512,8]{1,2,0:T(8,128)S(1)} fusion(bf16[2,512,1024]{2,1,0:T(8,128)(2,1)} %bitcast.187, pred[2,512]{1,0:T(4,128)(4,1)S(1)} %get-tuple-element.162, bf16[1024,8]{0,1:T(8,128)(2,1)S(1)} %copy-done.17, f32[8]{0:T(128)S(1)} %copy-done.18, f32[2,512]{1,0:T(2,128)S(1)} %get-tuple-element.161), kind=kOutput, calls=%fused_computation.80 | convolution fusion | flops 17891328 | bytes 2151456 | tf_op jit(solution)/shard_map/dot_general | solution.py:87
  28.4 3.5 %collective-permute-start.1 = (bf16[2,3,1280]{2,1,0:T(4,128)(2,1)S(1)}, bf16[2,3,1280]{2,1,0:T(4,128)(2,1)S(1)}, u32[]{:S(2)}, u32[]{:S(2)}) collective-permute-start(bf16[2,3,1280]{2,1,0:T(4,128)(2,1)S(1)} %collective-permute-done), channel_id=1, source_target_pairs={{0,2},{2,4},{4,6},{1,3},{3,5},{5,7},{8,10},{10,12},{12,14},{9,11},... | collective-permute-start | bytes 46088 | tf_op jit(solution)/shard_map/ppermute | solution.py:18
  33.3 6.3 %fusion.56 = (bf16[2,512,1280]{2,1,0:T(8,128)(2,1)S(1)}, f32[2,512,1280]{2,1,0:T(8,128)S(1)}) fusion(f32[1280]{0:T(1024)S(1)} %get-tuple-element.120, bf16[2,512,1280]{2,1,0:T(8,128)(2,1)} %bitcast.184, f32[1280]{0:T(1024)S(1)} %get-tuple-element.121, bf16[2,3,1280]{2,1,0:T(4,128)(2,1)S(1)} %select_select_fusion, f32[1280]{0:T(1024)S(1)} %get-tuple-element.119, ...), kind=kLoop, calls=%fused_computation.125 | loop fusion | flops 27525120 | bytes 10521600 | tf_op jit(solution)/shard_map/convert.10
  41.6 2.0 copy.91
  43.6 3.2 %copy.74 = bf16[2,4,128,8,128]{2,4,3,1,0:T(8,128)(2,1)S(1)} copy(bf16[2,4,128,8,128]{4,3,2,1,0:T(8,128)(2,1)} %bitcast.182) | data formatting | bytes 4194304 | tf_op jit(solution)/shard_map/reshape | solution.py:117
  46.8 2.3 %fusion.11 = f32[2,4,8,128,128]{4,3,2,1,0:T(8,128)S(1)} fusion(bf16[2,4,128,8,128]{2,4,3,1,0:T(8,128)(2,1)S(1)} %copy.74, f32[2,4,8,128]{3,2,1,0:T(8,128)S(1)} %exponential_multiply_fusion, f32[2,4,128,128]{3,2,1,0:T(8,128)S(1)} %convert_element_type.70), kind=kOutput, calls=%fused_computation.28 | convolution fusion | flops 270532608 | bytes 6848512 | tf_op jit(solution)/shard_map/schun,scuhp->schpn/dot_general | solution.py:134
  52.6 8.3 %all-gather = f32[8,1,8]{2,1,0:T(1,128)S(1)} all-gather(f32[2,1,8]{2,1,0:T(1,128)S(1)} %get-tuple-element.144), channel_id=2, replica_groups=mesh['row'=4,'col'=4,'batch'=2] {'row'}, dimensions={0}, use_global_device_ids=true | all-gather | bytes 320 | tf_op jit(solution)/shard_map/all_gather | solution.py:148
  60.9 45.4 %all-gather.4.cloned.1.call-done = f32[4,2,8,128,128]{4,3,2,1,0:T(8,128)} async-done(((f32[1,2,8,128,128]{4,3,2,1,0:T(8,128)}), f32[4,2,8,128,128]{4,3,2,1,0:T(8,128)}) %all-gather.4.cloned.1.call-update) | async-done | bytes 4194320 | tf_op jit(solution)/shard_map/all_gather | solution.py:149
  106.3 3.6 %multiply_add_fusion.1 = f32[1,2,8,128,128]{4,3,2,1,0:T(8,128)} fusion(f32[4,2,8,128,128]{4,3,2,1,0:T(8,128)} %all-gather.4.cloned.1.call-done, f32[2,8]{1,0:T(2,128)S(1)} %bitcast.201, f32[2,8]{1,0:T(2,128)S(1)} %get-tuple-element.156, f32[2,8]{1,0:T(2,128)S(1)} %get-tuple-element.157, f32[2,8]{1,0:T(2,128)S(1)} %get-tuple-element.158), kind=kLoop, calls=%fused_computation.71 | loop fusion | flops 1835008 | bytes 5243136 | tf_op jit(solution)/shard_map/add | solution.py:39
  110.1 4.6 %convolution_convert_fusion.1 = bf16[1024,1024]{1,0:T(8,128)(2,1)S(1)} fusion(bf16[1024,1024]{1,0:T(8,128)(2,1)} %param.18, bf16[1024,1024]{1,0:T(8,128)(2,1)} %gather_fusion, pred[1024]{0:T(1024)(128)(4,1)S(1)} %compare_and_fusion.1), kind=kOutput, calls=%fused_computation.44 | convolution fusion | flops 2149580800 | bytes 6292480 | tf_op jit(solution)/shard_map/dot_general | solution.py:83
  116.5 3.0 %copy.93 = f32[128,8,8,128]{3,2,1,0:T(8,128)} copy(f32[128,8,8,128]{3,1,2,0:T(8,128)S(1)} %convert_bitcast_fusion) | data formatting | bytes 8388608
  119.5 5.4 %copy.83 = f32[2,4,128,8,128]{2,4,3,1,0:T(8,128)} copy(f32[2,4,128,8,128]{4,3,2,1,0:T(8,128)} %bitcast.180) | data formatting | bytes 8388608 | tf_op jit(solution)/shard_map/convert_element_type | solution.py:170
  124.9 11.5 %all_gather.15 = f32[4,2,8]{2,1,0:T(2,128)S(1)} all-gather(f32[1,2,8]{2,1,0:T(2,128)S(1)} %bitcast.208), channel_id=1, replica_groups=mesh['row'=4,'col'=4,'batch'=2] {'col'}, dimensions={0}, use_global_device_ids=true | all-gather | bytes 320 | tf_op jit(solution)/shard_map/all_gather | solution.py:23
  136.7 4.4 %fusion.10 = f32[2,4,8,128,128]{4,3,2,1,0:T(8,128)} fusion(bf16[2,4,128,8,128]{2,4,3,1,0:T(8,128)(2,1)} %copy-done.6, f32[2,4,8,128]{3,2,1,0:T(8,128)S(1)} %bitcast.193, f32[2,4,8,128]{3,2,1,0:T(8,128)S(1)} %bitcast.192, f32[2,4,128,128]{3,2,1,0:T(8,128)S(1)} %fusion.58, pred[128,128]{1,0:T(8,128)(4,1)S(1)} %iota_compare_fusion), kind=kOutput, calls=%fused_computation.27 | convolution fusion | flops 275775488 | bytes 6897664 | tf_op jit(solution)/shard_map/schqu,scuhp->scqhp/dot_general | solution.py:129
  141.2 49.6 %all-gather.6.cloned.1.call-done = f32[4,2,8,128,128]{4,3,2,1,0:T(8,128)} async-done(((f32[1,2,8,128,128]{4,3,2,1,0:T(8,128)}), f32[4,2,8,128,128]{4,3,2,1,0:T(8,128)}) %all-gather.6.cloned.1.call-update) | async-done | bytes 4194320 | tf_op jit(solution)/shard_map/all_gather | solution.py:23
  190.8 6.0 %while.14 = (s32[]{:T(128)}, f32[2,8,128,128]{3,2,1,0:T(8,128)S(1)}, s32[]{:T(128)}, f32[4,2,8]{2,1,0:T(2,128)S(1)}, f32[4,2,8,128,128]{4,3,2,1,0:T(8,128)}, /*index=5*/s32[]{:T(128)}, s32[]{:T(128)}) while((s32[]{:T(128)}, f32[2,8,128,128]{3,2,1,0:T(8,128)S(1)}, s32[]{:T(128)}, f32[4,2,8]{2,1,0:T(2,128)S(1)}, ...), condition=%wide.region_2.3_spmd.clone, body=%wide.region_1.2_spmd.clone.sunk | while | flops 1048596 | bytes 3146025 | solution.py:35
  196.8 3.5 %convert_bitcast_fusion.1 = (bf16[2,1,8,128,128]{4,3,2,0,1:T(8,128)(2,1)S(1)}, f32[2,8,128,128]{3,2,1,0:T(8,128)S(1)}) fusion(f32[4,2,8,128,128]{4,3,2,1,0:T(8,128)} %all-gather.4.cloned.1.call-done, f32[2,8]{1,0:T(2,128)S(1)} %bitcast.202, pred[]{:T(512)S(6)} %gt.28, f32[2,8]{1,0:T(2,128)S(1)} %get-tuple-element.156, pred[]{:T(512)S(6)} %gt.27, ...), kind=kLoop, calls=%fused_computation.77 | loop fusion | flops 3670016 | bytes 6816068 | tf_op jit(solution)/shard_map/stack | solution.py:160
  202.9 3.1 %multiply_reduce_fusion = (f32[2,4,128]{2,1,0:T(4,128)S(1)}, f32[2,4,128,8,128]{2,4,3,1,0:T(8,128)}) fusion(f32[2,4,128,8,128]{2,4,3,1,0:T(8,128)S(1)} %copy-done.7, f32[2,4,128,8]{2,3,1,0:T(8,128)S(1)} %copy.80, bf16[2,4,128,128,1]{3,2,4,1,0:T(8,128)(2,1)S(1)} %bitcast.190, f32[2,4,8,128,128]{4,3,2,1,0:T(8,128)S(1)} %copy-done.19, ...), kind=kOutput, calls=%fused_computation.16 | convolution fusion | flops 281017344 | bytes 14979072 | tf_op jit(solution)/shard_map/scqn,schpn->scqhp/dot_general | solution.py:164
  206.0 5.4 %copy.81 = f32[2,4,128,8,128]{4,3,2,1,0:T(8,128)} copy(f32[2,4,128,8,128]{2,4,3,1,0:T(8,128)} %get-tuple-element.160) | data formatting | bytes 8388608 | tf_op jit(solution)/shard_map/add | solution.py:169
  211.5 4.1 %fusion.7 = bf16[1024,1024]{1,0:T(8,128)(2,1)S(1)} fusion(bf16[1024,1024]{1,0:T(8,128)(2,1)S(1)} %copy-done.5, f32[128,8,8,128]{3,2,1,0:T(8,128)} %bitcast.179, f32[1024]{0:T(1024)S(1)} %copy-done.12, f32[1024]{0:T(1024)S(1)} %bitcast.195), kind=kLoop, calls=%fused_computation.20 | loop fusion | flops 9437184 | bytes 8396800 | tf_op jit(solution)/shard_map/convert_element_type | solution.py:175
  215.7 3.7 %fusion.25 = bf16[2,1,512,1024]{3,2,1,0:T(8,128)(2,1)} fusion(f32[2,512]{1,0:T(2,128)S(1)} %get-tuple-element.161, bf16[2,512,1024]{2,1,0:T(8,128)(2,1)S(1)} %bitcast.188, bf16[1024,1024]{1,0:T(8,128)(2,1)S(1)} %copy-done.16), kind=kOutput, calls=%fused_computation.45 | convolution fusion | flops 2149580800 | bytes 6295552 | tf_op jit(solution)/shard_map/dot_general | solution.py:176
  (86 shorter events, 22.1 us)
Async XLA Ops:
  6.5 8.9 %copy-start = (bf16[1024,1280]{1,0:T(8,128)(2,1)S(1)}, bf16[1024,1280]{1,0:T(8,128)(2,1)}, u32[]{:S(2)}) copy-start(bf16[1024,1280]{1,0:T(8,128)(2,1)} %param.19) | copy-start | bytes 7864324
  6.5 99.7 %all-gather.4.cloned.1.call-start = ((), (), s32[]{:S(2)}) async-start(), calls=%async_computation | async-start | bytes 5242880 | tf_op jit(solution)/shard_map/all_gather | solution.py:149
  15.5 9.2 %copy-start.13 = (s32[2,1,512]{2,1,0:T(1,128)S(1)}, s32[2,1,512]{2,1,0:T(1,128)}, u32[]{:S(2)}) copy-start(s32[2,1,512]{2,1,0:T(1,128)} %param.15) | copy-start | bytes 12292
  15.5 9.2 %copy-start.10 = (s32[2,1,512]{2,1,0:T(1,128)S(1)}, s32[2,1,512]{2,1,0:T(1,128)}, u32[]{:S(2)}) copy-start(s32[2,1,512]{2,1,0:T(1,128)} %param.14) | copy-start | bytes 12292
  15.5 9.2 %copy-start.15 = (s32[2]{0:T(128)S(1)}, s32[2]{0:T(128)}, u32[]{:S(2)}) copy-start(s32[2]{0:T(128)} %param.16) | copy-start | bytes 28
  15.5 9.3 %copy-start.17 = (bf16[1024,8]{0,1:T(8,128)(2,1)S(1)}, bf16[1024,8]{0,1:T(8,128)(2,1)}, u32[]{:S(2)}) copy-start(bf16[1024,8]{0,1:T(8,128)(2,1)} %param.20) | copy-start | bytes 49156
  15.5 9.2 %copy-start.18 = (f32[8]{0:T(128)S(1)}, f32[8]{0:T(128)}, u32[]{:S(2)}) copy-start(f32[8]{0:T(128)} %param.22) | copy-start | bytes 100
  15.5 11.6 %copy-start.14 = (f32[8]{0:T(128)S(1)}, f32[8]{0:T(128)}, u32[]{:S(2)}) copy-start(f32[8]{0:T(128)} %param.23) | copy-start | bytes 100
  20.1 1.5 copy-start.8
  20.1 11.8 %copy-start.11 = (f32[4,1280]{1,0:T(4,128)S(1)}, f32[4,1280]{1,0:T(4,128)}, u32[]{:S(2)}) copy-start(f32[4,1280]{1,0:T(4,128)} %param.21) | copy-start | bytes 61444
  21.6 6.8 %collective-permute-start = (bf16[2,3,1280]{2,1,0:T(4,128)(2,1)S(1)}, bf16[2,3,1280]{2,1,0:T(4,128)(2,1)S(1)}, u32[]{:S(2)}, u32[]{:S(2)}) collective-permute-start(bf16[2,3,1280]{2,1,0:T(4,128)(2,1)S(1)} %slice.121), channel_id=1, source_target_pairs={{24,0},{0,8},{8,16},{16,24},{25,1},{1,9},{9,17},{17,25},{26,2},{2,... | collective-permute-start | bytes 46088 | tf_op jit(solution)/shard_map/ppermute | solution.py:12
  28.4 5.0 %collective-permute-start.1 = (bf16[2,3,1280]{2,1,0:T(4,128)(2,1)S(1)}, bf16[2,3,1280]{2,1,0:T(4,128)(2,1)S(1)}, u32[]{:S(2)}, u32[]{:S(2)}) collective-permute-start(bf16[2,3,1280]{2,1,0:T(4,128)(2,1)S(1)} %collective-permute-done), channel_id=1, source_target_pairs={{0,2},{2,4},{4,6},{1,3},{3,5},{5,7},{8,10},{10,12},{12,14},{9,11},... | collective-permute-start | bytes 46088 | tf_op jit(solution)/shard_map/ppermute | solution.py:18
  46.8 5.7 %copy-start.6 = (bf16[2,4,128,8,128]{2,4,3,1,0:T(8,128)(2,1)}, bf16[2,4,128,8,128]{2,4,3,1,0:T(8,128)(2,1)S(1)}, u32[]{:S(2)}) copy-start(bf16[2,4,128,8,128]{2,4,3,1,0:T(8,128)(2,1)S(1)} %copy.74) | copy-start | bytes 6291460
  49.0 2.0 copy-start.2
  52.5 138.3 %all-gather.6.cloned.1.call-start = ((), (), s32[]{:S(2)}) async-start(), calls=%async_computation.1 | async-start | bytes 5242880 | tf_op jit(solution)/shard_map/all_gather | solution.py:23
  114.8 1.3 copy-start.4
  119.5 16.9 %copy-start.9 = (bf16[2,512,128]{2,1,0:T(8,128)(2,1)S(1)}, bf16[2,512,128]{2,1,0:T(8,128)(2,1)}, u32[]{:S(2)}) copy-start(bf16[2,512,128]{2,1,0:T(8,128)(2,1)} %get-tuple-element.142) | copy-start | bytes 786436
  196.8 3.5 %copy-start.3 = (f32[2,4,8,128,128]{4,3,2,1,0:T(8,128)S(1)}, f32[2,4,8,128,128]{4,3,2,1,0:T(8,128)}, u32[]{:S(2)}) copy-start(f32[2,4,8,128,128]{4,3,2,1,0:T(8,128)} %copy-done.2) | copy-start | bytes 12582916
  196.8 4.7 %copy-start.19 = (f32[2,4,8,128,128]{4,3,2,1,0:T(8,128)S(1)}, f32[2,4,8,128,128]{4,3,2,1,0:T(8,128)}, u32[]{:S(2)}) copy-start(f32[2,4,8,128,128]{4,3,2,1,0:T(8,128)} %fusion.10) | copy-start | bytes 12582916
  200.3 2.6 %copy-start.7 = (f32[2,4,128,8,128]{2,4,3,1,0:T(8,128)S(1)}, f32[2,4,128,8,128]{2,4,3,1,0:T(8,128)}, u32[]{:S(2)}) copy-start(f32[2,4,128,8,128]{2,4,3,1,0:T(8,128)} %copy.83) | copy-start | bytes 12582916
  206.0 5.5 %copy-start.5 = (bf16[1024,1024]{1,0:T(8,128)(2,1)S(1)}, bf16[1024,1024]{1,0:T(8,128)(2,1)}, u32[]{:S(2)}) copy-start(bf16[1024,1024]{1,0:T(8,128)(2,1)} %copy-done.4) | copy-start | bytes 6291460
  206.0 5.5 %copy-start.12 = (f32[1024]{0:T(1024)S(1)}, f32[1024]{0:T(1024)}, u32[]{:S(2)}) copy-start(f32[1024]{0:T(1024)} %param.24) | copy-start | bytes 12292
  211.5 4.2 %copy-start.16 = (bf16[1024,1024]{1,0:T(8,128)(2,1)S(1)}, bf16[1024,1024]{1,0:T(8,128)(2,1)}, u32[]{:S(2)}) copy-start(bf16[1024,1024]{1,0:T(8,128)(2,1)} %param.25) | copy-start | bytes 6291460
  215.6 3.7 %copy-start.1 = (bf16[1024,1280]{1,0:T(8,128)(2,1)S(1)}, bf16[1024,1280]{1,0:T(8,128)(2,1)}, u32[]{:S(2)}) copy-start(bf16[1024,1280]{1,0:T(8,128)(2,1)} %param.19) | copy-start | bytes 7864324
Sparse Core Ops, SparseCore 0:
  52.6 53.6 all-gather.3
  110.0 80.7 all-gather.5
where the time goes:
time: 227 us; the launch traced here: 226 us
  waiting for transfers between devices  96.5 us (43%)
  local copies, waits for them, and re-layouts  34.6 us (15%)
  other arithmetic  29.7 us (13%)
  matrix products  25.3 us (11%)
  blocking collectives  19.8 us (9%)
  between operations  13.8 us (6%)
  starting transfers between devices  6.55 us (3%)
    all_gather x1, waiting for transfers between devices, carried_in(): everything = jax.tree.map(lambda part: lax.all_gather(part, axis), shard)  49.6 us
    all_gather x1, waiting for transfers between devices, per_device(): lax.all_gather(running[1][None], 'row', axis=0, tiled=True)  45.4 us
    unnamed x42, local copies, waits for them, and re-layouts  11.6 us
    all_gather x1, blocking collectives, carried_in(): everything = jax.tree.map(lambda part: lax.all_gather(part, axis), shard)  11.5 us
    all_gather x1, blocking collectives, per_device(): lax.all_gather(running[0][None], 'row', axis=0, tiled=True)  8.27 us
    gather x1, local copies, waits for them, and re-layouts, per_device(): jnp.take(item_table, item_rows, axis=0).reshape(users * events, -1)  7.37 us
    another operation x1, other arithmetic  6.32 us
    select_n x4, other arithmetic, lap(): return jax.tree.map(lambda a, b: jnp.where(reached, a, b), new, before)  5.83 us
  transfers between devices with their start and end apart: 4, of which 3 were waited for; matrix products, arithmetic and copies ran while one was open for 10% of the time, Pallas kernels for 0%

commit v1 on v0

v1 whole, which is shorter than its diff:
```python
import functools

import jax
import jax.numpy as jnp
from jax import lax
from jax.experimental import pallas as pl
from jax.experimental.pallas import tpu as pltpu
from jax.sharding import PartitionSpec as P

STRETCH = 128
LANES = 128
HALO = 16
MESH = pl.DeviceIdType.MESH
F32 = jnp.float32
BF16 = jnp.bfloat16


def silu(v):
    return 0.5 * v * (1.0 + jnp.tanh(0.5 * v))


def local_kernel(
    counts,
    meta_ref,
    tin_ref,
    tgate_ref,
    tdt_ref,
    taps_ref,
    bias_ref,
    rates_ref,
    y_ref,
    gate_ref,
    out_ref,
    ef_ref,
    state_ref,
    log_ref,
    pbuf,
    scaled,
    run,
    cum,
):
    stretch_count, head_count, head_size, state_width, pieces = counts
    inner = head_count * head_size
    place = lax.rem(pl.program_id(0), stretch_count)

    @pl.when(place == 0)
    def _():
        run[...] = jnp.zeros_like(run)
        cum[...] = jnp.zeros_like(cum)

    meta = jnp.transpose(meta_ref[0])
    ids = meta[: HALO + STRETCH, 0:1].astype(jnp.int32)
    usable = meta[:STRETCH, 1:2]
    items = tin_ref.shape[0]
    hot = (ids == lax.broadcasted_iota(jnp.int32, (HALO + STRETCH, items), 1)).astype(F32).astype(BF16)
    pbuf[...] = jnp.dot(hot, tin_ref[...], preferred_element_type=F32)
    now = hot[HALO:]
    gate_ref[...] = jnp.dot(now, tgate_ref[...], preferred_element_type=F32).astype(BF16)
    parts = jnp.dot(now, tdt_ref[...], preferred_element_type=F32)
    raw = (
        parts
        + pltpu.roll(parts, LANES - head_count, 1)
        + pltpu.roll(parts, LANES - 2 * head_count, 1)
    )
    raw = raw + bias_ref[...]
    step = usable * (jnp.maximum(raw, 0.0) + jnp.log1p(jnp.exp(-jnp.abs(raw))))
    rows = lax.broadcasted_iota(jnp.int32, (STRETCH, STRETCH), 0)
    cols = lax.broadcasted_iota(jnp.int32, (STRETCH, STRETCH), 1)
    causal = rows >= cols
    logs = jnp.dot(
        jnp.where(causal, 1.0, 0.0).astype(F32),
        step * rates_ref[...],
        precision=lax.Precision.HIGHEST,
        preferred_element_type=F32,
    )
    total = logs[STRETCH - 1 :, :]
    logs_t = jnp.transpose(logs)
    step_t = jnp.transpose(step)
    kernel = taps_ref.shape[0]
    conv = None
    for k in range(kernel):
        start = HALO - (kernel - 1) + k
        term = pbuf[start : start + STRETCH, :] * taps_ref[k : k + 1, :]
        conv = term if conv is None else conv + term
    signal = silu(conv[:, :inner]).astype(BF16)
    inward = conv[:, inner : inner + state_width].astype(BF16)
    outward = conv[:, inner + state_width :].astype(BF16)
    out_ref[...] = outward
    scores = lax.dot_general(
        outward, inward, (((1,), (1,)), ((), ())), preferred_element_type=F32
    )
    scores = jnp.where(causal, scores, 0.0)
    tail = jnp.exp(logs - total) * step
    fade = jnp.exp(-logs)
    held = jnp.dot(outward, run[...].astype(BF16), preferred_element_type=F32)
    for h in range(head_count):
        span = slice(h * head_size, (h + 1) * head_size)
        gap = jnp.minimum(logs_t[h : h + 1, :] - logs[:, h : h + 1], 0.0)
        weights = (jnp.exp(gap) * (scores * step_t[h : h + 1, :])).astype(BF16)
        near = jnp.dot(weights, signal[:, span], preferred_element_type=F32)
        y_ref[:, span] = near + held[:, span] * fade[:, h : h + 1]
        scaled[:, span] = (signal[:, span].astype(F32) * tail[:, h : h + 1]).astype(BF16)
    added = lax.dot_general(
        inward, scaled[...], (((0,), (0,)), ((), ())), preferred_element_type=F32
    )
    shrink = jnp.exp(-total)
    for h in range(head_count):
        span = slice(h * head_size, (h + 1) * head_size)
        run[:, span] = run[:, span] * shrink[:, h : h + 1] + added[:, span]
    before = cum[0:1, :]
    lane = lax.broadcasted_iota(jnp.int32, (STRETCH, LANES), 1)
    ef_ref[...] = jnp.where(lane == LANES - 1, usable, jnp.exp(-(logs + before)))
    after = before + total
    cum[...] = jnp.broadcast_to(after, cum.shape)

    @pl.when(place == stretch_count - 1)
    def _():
        width = inner // pieces
        for q in range(pieces):
            state_ref[q, 0] = run[:, q * width : (q + 1) * width].astype(BF16)
            for j in range(width // head_size):
                h = q * (width // head_size) + j
                log_ref[q, 0, :, j * head_size : (j + 1) * head_size] = jnp.broadcast_to(
                    after[:, h : h + 1], (8, head_size)
                )


def chain_kernel(
    rows,
    cols,
    state_ref,
    log_ref,
    enter_ref,
    rin,
    lin,
    before,
    fades,
    pin,
    psend,
    esend,
    s1,
    r1,
    sl,
    rl,
    s2,
    r2,
    s3,
    r3,
):
    users = state_ref.shape[1]
    r, c = lax.axis_index("row"), lax.axis_index("col")
    barrier = pltpu.get_barrier_semaphore()
    for d in range(1, rows):
        pl.semaphore_signal(
            barrier, inc=1, device_id={"row": lax.rem(r + d, rows)}, device_id_type=MESH
        )

    @pl.when(c > 0)
    def _():
        pl.semaphore_signal(barrier, inc=1, device_id={"col": c - 1}, device_id_type=MESH)

    @pl.when(c < cols - 1)
    def _():
        pl.semaphore_signal(barrier, inc=1, device_id={"col": c + 1}, device_id_type=MESH)

    peers = rows - 1 + jnp.where(c > 0, 1, 0) + jnp.where(c < cols - 1, 1, 0)
    pl.semaphore_wait(barrier, peers)

    first = []
    for d in range(1, rows):
        q = lax.rem(r + d, rows)
        for source, target, send, recv in (
            (log_ref, lin, sl, rl),
            (state_ref, rin, s1, r1),
        ):
            copy = pltpu.make_async_remote_copy(
                src_ref=source.at[q],
                dst_ref=target.at[r],
                send_sem=send.at[d],
                recv_sem=recv.at[d],
                device_id={"row": q},
                device_id_type=MESH,
            )
            copy.start()
            first.append(copy)
    rin[r] = state_ref[r]
    lin[r] = log_ref[r]
    for copy in first:
        copy.wait()

    for u in range(users):
        carried = jnp.zeros(pin.shape[1:], F32)
        fade = jnp.ones((1, pin.shape[2]), F32)
        for m in range(rows):
            before[m, u] = carried
            fades[m, u] = jnp.broadcast_to(fade, fades.shape[2:])
            here = jnp.exp(-lin[m, u, 0:1, :])
            carried = here * carried + rin[m, u].astype(F32)
            fade = fade * here
        before[rows, u] = carried
        fades[rows, u] = jnp.broadcast_to(fade, fades.shape[2:])

    @pl.when(c == 0)
    def _():
        pin[...] = jnp.zeros_like(pin)

    second = []
    third = []
    for u in range(users):
        copy = pltpu.make_async_remote_copy(
            src_ref=psend.at[u],
            dst_ref=pin.at[u],
            send_sem=s2.at[u],
            recv_sem=r2.at[u],
            device_id={"col": lax.rem(c + 1, cols)},
            device_id_type=MESH,
        )
        second.append(copy)

        @pl.when(c > 0)
        def _(copy=copy):
            copy.wait_recv()

        @pl.when(c < cols - 1)
        def _(copy=copy, u=u):
            psend[u] = (fades[rows, u, 0:1, :] * pin[u].astype(F32) + before[rows, u]).astype(BF16)
            copy.start()

        for d in range(1, rows):
            q = lax.rem(r + d, rows)
            esend[d, u] = (fades[q, u, 0:1, :] * pin[u].astype(F32) + before[q, u]).astype(BF16)
            copy = pltpu.make_async_remote_copy(
                src_ref=esend.at[d, u],
                dst_ref=enter_ref.at[r, u],
                send_sem=s3.at[d, u],
                recv_sem=r3.at[d, u],
                device_id={"row": q},
                device_id_type=MESH,
            )
            copy.start()
            third.append(copy)
        enter_ref[r, u] = (fades[r, u, 0:1, :] * pin[u].astype(F32) + before[r, u]).astype(BF16)
    for copy in third:
        copy.wait()

    @pl.when(c < cols - 1)
    def _():
        for copy in second:
            copy.wait_send()


def finish_kernel(
    head_count, y_ref, gate_ref, outward_ref, ef_ref, enter_ref, gain_ref, wout_ref, result_ref, mix
):
    pieces, _, _, width = enter_ref.shape
    inner = pieces * width
    head_size = inner // head_count
    squares = None
    for q in range(pieces):
        far = jnp.dot(outward_ref[...], enter_ref[q, 0], preferred_element_type=F32)
        for j in range(width // head_size):
            h = q * (width // head_size) + j
            span = slice(h * head_size, (h + 1) * head_size)
            both = y_ref[:, span] + far[:, j * head_size : (j + 1) * head_size] * ef_ref[:, h : h + 1]
            value = both * silu(gate_ref[:, span].astype(F32))
            mix[:, span] = value
            squares = value * value if squares is None else squares + value * value
    mean = jnp.sum(squares, axis=1, keepdims=True) * (1.0 / inner)
    normed = (mix[...] * lax.rsqrt(mean + 1.0) * gain_ref[...]).astype(BF16)
    result = jnp.dot(normed, wout_ref[...], preferred_element_type=F32)
    result_ref[...] = (result * ef_ref[:, LANES - 1 : LANES]).astype(BF16)


def per_device(
    item_ids,
    pad_masks,
    lengths,
    item_table,
    w_gate,
    w_in,
    w_dt,
    conv_taps,
    dt_bias,
    decay_rates,
    norm_gain,
    w_out,
):
    users = item_ids.shape[0]
    events = item_ids.shape[2]
    items, model = item_table.shape
    full_width = w_in.shape[1]
    inner = w_gate.shape[1]
    head_count = decay_rates.shape[0]
    head_size = inner // head_count
    state_width = (full_width - inner) // 2
    rows, cols = lax.axis_size("row"), lax.axis_size("col")
    row_place, col_place = lax.axis_index("row"), lax.axis_index("col")
    stretch_count = events // STRETCH
    steps = users * stretch_count
    width = inner // rows

    item_rows = item_ids[:, 0, :]
    order = [r * cols + c for c in range(cols) for r in range(rows)]
    route = list(zip(order[:-1], order[1:]))
    halo = lax.ppermute(item_rows[:, events - HALO :] + 1, ("row", "col"), route) - 1
    first_event = (col_place * rows + row_place) * events
    position = first_event + lax.broadcasted_iota(jnp.int32, (users, events), 1)
    usable = jnp.logical_and(position < lengths[:, None], pad_masks[:, 0, :] > 0)
    joined = jnp.concatenate([halo, item_rows], axis=1).astype(F32)
    padded = 2 * STRETCH
    windows = jnp.stack(
        [joined[:, c * STRETCH : c * STRETCH + HALO + STRETCH] for c in range(stretch_count)], axis=1
    )
    windows = jnp.pad(windows, ((0, 0), (0, 0), (0, padded - HALO - STRETCH)))
    flags = jnp.pad(
        usable.astype(F32).reshape(users, stretch_count, STRETCH),
        ((0, 0), (0, 0), (0, padded - STRETCH)),
    )
    meta = jnp.pad(jnp.stack([windows, flags], axis=2), ((0, 0), (0, 0), (0, 6), (0, 0)))
    meta = meta.reshape(steps, 8, padded)

    table_in = jnp.dot(item_table, w_in, preferred_element_type=F32).astype(BF16)
    table_gate = jnp.dot(item_table, w_gate, preferred_element_type=F32).astype(BF16)
    raw = jnp.dot(item_table, w_dt, preferred_element_type=F32)
    high = lax.reduce_precision(raw, 8, 7)
    middle = lax.reduce_precision(raw - high, 8, 7)
    low = raw - high - middle
    table_dt = jnp.concatenate([high, middle, low], axis=1).astype(BF16)
    table_dt = jnp.pad(table_dt, ((0, 0), (0, LANES - 3 * head_count)))
    bias = jnp.pad(dt_bias[None], ((0, 0), (0, LANES - head_count)))
    rates = jnp.pad(decay_rates[None], ((0, 0), (0, LANES - head_count)))

    def whole(shape):
        return pl.BlockSpec(shape, lambda s: (0,) * len(shape))

    def by_rows(columns):
        return pl.BlockSpec((STRETCH, columns), lambda s: (s, 0))

    total_rows = users * events
    y, gate, outward, ef, state, logs = pl.pallas_call(
        functools.partial(
            local_kernel, (stretch_count, head_count, head_size, state_width, rows)
        ),
        grid=(steps,),
        in_specs=[
            pl.BlockSpec((1, 8, padded), lambda s: (s, 0, 0)),
            whole((items, full_width)),
            whole((items, inner)),
            whole((items, LANES)),
            whole(conv_taps.shape),
            whole((1, LANES)),
            whole((1, LANES)),
        ],
        out_specs=[
            by_rows(inner),
            by_rows(inner),
            by_rows(state_width),
            by_rows(LANES),
            pl.BlockSpec((rows, 1, state_width, width), lambda s: (0, s // stretch_count, 0, 0)),
            pl.BlockSpec((rows, 1, 8, width), lambda s: (0, s // stretch_count, 0, 0)),
        ],
        out_shape=[
            jax.ShapeDtypeStruct((total_rows, inner), F32),
            jax.ShapeDtypeStruct((total_rows, inner), BF16),
            jax.ShapeDtypeStruct((total_rows, state_width), BF16),
            jax.ShapeDtypeStruct((total_rows, LANES), F32),
            jax.ShapeDtypeStruct((rows, users, state_width, width), BF16),
            jax.ShapeDtypeStruct((rows, users, 8, width), F32),
        ],
        scratch_shapes=[
            pltpu.VMEM((HALO + STRETCH, full_width), F32),
            pltpu.VMEM((STRETCH, inner), BF16),
            pltpu.VMEM((state_width, inner), F32),
            pltpu.VMEM((8, LANES), F32),
        ],
        compiler_params=pltpu.CompilerParams(dimension_semantics=("arbitrary",)),
        name="local_part",
    )(meta, table_in, table_gate, table_dt, conv_taps, bias, rates)

    vmem = pl.BlockSpec(memory_space=pltpu.VMEM)
    dma = pltpu.SemaphoreType.DMA
    entering = pl.pallas_call(
        functools.partial(chain_kernel, rows, cols),
        in_specs=[vmem, vmem],
        out_specs=vmem,
        out_shape=jax.ShapeDtypeStruct(state.shape, BF16),
        scratch_shapes=[
            pltpu.VMEM(state.shape, BF16),
            pltpu.VMEM(logs.shape, F32),
            pltpu.VMEM((rows + 1,) + state.shape[1:], F32),
            pltpu.VMEM((rows + 1,) + logs.shape[1:], F32),
            pltpu.VMEM(state.shape[1:], BF16),
            pltpu.VMEM(state.shape[1:], BF16),
            pltpu.VMEM(state.shape, BF16),
            dma((rows,)),
            dma((rows,)),
            dma((rows,)),
            dma((rows,)),
            dma((users,)),
            dma((users,)),
            dma((rows, users)),
            dma((rows, users)),
        ],
        compiler_params=pltpu.CompilerParams(collective_id=0, has_side_effects=True),
        name="state_chain",
    )(state, logs)

    result = pl.pallas_call(
        functools.partial(finish_kernel, head_count),
        grid=(steps,),
        in_specs=[
            by_rows(inner),
            by_rows(inner),
            by_rows(state_width),
            by_rows(LANES),
            pl.BlockSpec((rows, 1, state_width, width), lambda s: (0, s // stretch_count, 0, 0)),
            whole((1, inner)),
            whole(w_out.shape),
        ],
        out_specs=by_rows(w_out.shape[1]),
        out_shape=jax.ShapeDtypeStruct((total_rows, w_out.shape[1]), BF16),
        scratch_shapes=[pltpu.VMEM((STRETCH, inner), F32)],
        compiler_params=pltpu.CompilerParams(dimension_semantics=("arbitrary",)),
        name="finish_part",
    )(y, gate, outward, ef, entering, norm_gain[None], w_out)
    return result.reshape(users, 1, events, -1)


def solution(mesh):
    in_specs = (
        P("batch", "col", "row"),
        P("batch", "col", "row"),
        P("batch"),
        P(),
        P(),
        P(),
        P(),
        P(),
        P(),
        P(),
        P(),
        P(),
    )
    out_specs = P("batch", "col", "row", None)
    return jax.shard_map(
        per_device, mesh=mesh, in_specs=in_specs, out_specs=out_specs, check_vma=False
    )
```

time: 227 us -> 74.5 us (0.33)
  the two profiles are of different devices: /device:TPU:0 before, /device:TPU:24 now
where the time goes in v1:
time: 74.5 us; the launch traced here: 74.1 us
  Pallas kernels  55.9 us (75%)
  matrix products  8.44 us (11%)
  local copies, waits for them, and re-layouts  4.63 us (6%)
  starting transfers between devices  3.39 us (5%)
  other arithmetic  1.65 us (2%)
    pallas_call x1, Pallas kernels, per_device(): pl.pallas_call(functools.partial(chain_kernel, rows, cols), in_specs=[vme...  26.4 us
    pallas_call x1, Pallas kernels, per_device(): pl.pallas_call(functools.partial(local_kernel, (stretch_count, head_count...  18.8 us
    pallas_call x1, Pallas kernels, per_device(): pl.pallas_call(functools.partial(finish_kernel, head_count), grid=(steps,...  10.7 us
    dot_general x1, matrix products, per_device(): jnp.dot(item_table, w_gate, preferred_element_type=F32).astype(BF16)  4.25 us
    ppermute x1, starting transfers between devices, per_device(): lax.ppermute(item_rows[:, events - HALO:] + 1, ('row', 'col'), route) - 1  3.39 us
    dot_general x1, matrix products, per_device(): jnp.dot(item_table, w_in, preferred_element_type=F32).astype(BF16)  2.59 us
    dot_general x1, matrix products, per_device(): raw = jnp.dot(item_table, w_dt, preferred_element_type=F32)  1.6 us
  transfers between devices with their start and end apart: 1, of which 0 were waited for; matrix products, arithmetic and copies ran while one was open for 18% of the time, Pallas kernels for 0%

profile of v1, /device:TPU:24, one launch (start us, length us, event | category | flops | bytes accessed | tf_op | source)
XLA Modules:
  0.0 74.1 jit_solution(774639081284021506)
XLA Ops:
  0.0 0.0 copy-start
  0.0 0.8 %copy.25 = s32[2,1,512]{2,0,1:T(2,128)S(1)} copy(s32[2,1,512]{2,1,0:T(1,128)} %param.12) | data formatting | bytes 8192
  0.8 0.1 slice_add_fusion
  0.9 3.4 %collective-permute-start = (s32[2,16]{1,0:T(2,128)S(1)}, s32[2,16]{1,0:T(2,128)S(1)}, u32[]{:S(2)}, u32[]{:S(2)}) collective-permute-start(s32[2,16]{1,0:T(2,128)S(1)} %slice_add_fusion), channel_id=1, source_target_pairs={{0,8},{8,16},{16,24},{24,2},{2,10},{10,18},{18,26},{26,4},{4,12},{... | collective-permute-start | bytes 392 | tf_op jit(solution)/shard_map/ppermute | solution.py:305
  4.3 1.2 %pad.28.bias_ref = f32[1,128]{1,0:T(1,128)} pad(f32[1,8]{1,0:T(1,128)} %bitcast.34, f32[]{:T(128)} %constant.19.clone.1), padding=0_0x0_120 | pad | bytes 548 | tf_op jit(solution)/shard_map/jit(_pad)/pad | solution.py:330
  5.5 1.1 %pad.29.rates_ref = f32[1,128]{1,0:T(1,128)} pad(f32[1,8]{1,0:T(1,128)} %bitcast.35, f32[]{:T(128)} %constant.19.clone.1), padding=0_0x0_120 | pad | bytes 548 | tf_op jit(solution)/shard_map/jit(_pad)/pad | solution.py:331
  6.7 0.7 compare_reduce_fusion
  7.4 0.7 bitcast_and_fusion
  8.1 1.6 %reduce-precision_convert_fusion.1 = (bf16[512,8]{0,1:T(8,128)(2,1)S(1)}, bf16[512,8]{0,1:T(8,128)(2,1)S(1)}, bf16[512,8]{0,1:T(8,128)(2,1)S(1)}) fusion(bf16[512,1024]{1,0:T(8,128)(2,1)} %param.15, bf16[1024,8]{0,1:T(8,128)(2,1)} %param.18), kind=kOutput, calls=%fused_computation.6 | convolution fusion | flops 8417280 | bytes 1089536 | tf_op jit(solution)/shard_map/dot_general | solution.py:324
  9.7 0.1 copy.20
  9.9 0.0 copy-start.1
  9.9 4.2 %convolution_convert_fusion.1.tgate_ref = bf16[512,1024]{1,0:T(8,128)(2,1)} fusion(bf16[512,1024]{1,0:T(8,128)(2,1)} %param.15, bf16[1024,1024]{1,0:T(8,128)(2,1)} %param.16), kind=kOutput, calls=%fused_computation.1 | convolution fusion | flops 1074266112 | bytes 4194304 | tf_op jit(solution)/shard_map/dot_general | solution.py:323
  14.1 0.0 copy-done
  14.1 0.0 copy-done.1
  14.1 2.6 %convolution_convert_fusion.tin_ref = bf16[512,1280]{1,0:T(8,128)(2,1)} fusion(bf16[512,1024]{1,0:T(8,128)(2,1)S(1)} %copy-done.1, bf16[1024,1280]{1,0:T(8,128)(2,1)S(1)} %copy-done), kind=kOutput, calls=%fused_computation | convolution fusion | flops 1342832640 | bytes 4980736 | tf_op jit(solution)/shard_map/dot_general | solution.py:322
  16.7 0.7 pad.27.tdt_ref
  17.4 0.0 collective-permute-done
  17.4 0.1 add_convert_fusion
  17.5 0.6 pad.26.clone
  18.2 18.8 %local_part.1 = (f32[1024,1024]{1,0:T(8,128)}, bf16[1024,1024]{1,0:T(8,128)(2,1)}, bf16[1024,128]{1,0:T(8,128)(2,1)}, f32[1024,128]{1,0:T(8,128)}, bf16[4,2,128,...) custom-call(f32[8,8,256]{2,1,0:T(8,128)} %bitcast.30, bf16[512,1280]{1,0:T(8,128)(2,1)} %convolution_convert_fusion.tin_ref, ...), custom_call_target="tpu_custom_call" | custom-call | tf_op jit(solution)/shard_map/local_part/pallas_call | solution.py:340
  37.0 26.4 %state_chain.1.enter_ref = bf16[4,2,128,256]{3,2,1,0:T(8,128)(2,1)} custom-call(bf16[4,2,128,256]{3,2,1,0:T(8,128)(2,1)} %get-tuple-element.15.state_ref, f32[4,2,8,256]{3,2,1,0:T(8,128)} %get-tuple-element.16.log_ref), custom_call_target="tpu_custom_call" | custom-call | tf_op jit(solution)/shard_map/state_chain/pallas_call | solution.py:382
  63.4 10.7 %finish_part.1 = bf16[1024,1024]{1,0:T(8,128)(2,1)} custom-call(f32[1024,1024]{1,0:T(8,128)} %get-tuple-element.11.y_ref, bf16[1024,1024]{1,0:T(8,128)(2,1)} %get-tuple-element.12.gate_ref, bf16[1024,128]{1,0:T(8,128)(2,1)} %get-tuple-element.13.outward_ref, f32[1024,128]{1,0:T(8,128)} %get-tuple-element.14.ef_ref, ...), custom_call_target="tpu_custom_call" | custom-call | tf_op jit(solution)/shard_map/finish_part/pallas_call | solution.py:408
  (8 shorter events, 0.1 us)
Async XLA Ops:
  0.0 14.1 %copy-start = (bf16[1024,1280]{1,0:T(8,128)(2,1)S(1)}, bf16[1024,1280]{1,0:T(8,128)(2,1)}, u32[]{:S(2)}) copy-start(bf16[1024,1280]{1,0:T(8,128)(2,1)} %param.17) | copy-start | bytes 7864324
  0.9 16.5 %collective-permute-start = (s32[2,16]{1,0:T(2,128)S(1)}, s32[2,16]{1,0:T(2,128)S(1)}, u32[]{:S(2)}, u32[]{:S(2)}) collective-permute-start(s32[2,16]{1,0:T(2,128)S(1)} %slice_add_fusion), channel_id=1, source_target_pairs={{0,8},{8,16},{16,24},{24,2},{2,10},{10,18},{18,26},{26,4},{4,12},{... | collective-permute-start | bytes 392 | tf_op jit(solution)/shard_map/ppermute | solution.py:305
  9.9 4.3 %copy-start.1 = (bf16[512,1024]{1,0:T(8,128)(2,1)S(1)}, bf16[512,1024]{1,0:T(8,128)(2,1)}, u32[]{:S(2)}) copy-start(bf16[512,1024]{1,0:T(8,128)(2,1)} %param.15) | copy-start | bytes 3145732

commit v2 on v1

--- a/solution.py
+++ b/solution.py
@@ -19,9 +19,43 @@
     return 0.5 * v * (1.0 + jnp.tanh(0.5 * v))
 
 
+def project_kernel(
+    counts, table_ref, win_ref, wgate_ref, wdt_ref, tin_ref, tgate_ref, tdt_ref, wide
+):
+    in_blocks, gate_blocks, head_count = counts
+    step = pl.program_id(0)
+
+    @pl.when(step < in_blocks)
+    def _():
+        tin_ref[...] = jnp.dot(
+            table_ref[...], win_ref[...], preferred_element_type=F32
+        ).astype(BF16)
+
+    @pl.when(step < gate_blocks)
+    def _():
+        tgate_ref[...] = jnp.dot(
+            table_ref[...], wgate_ref[...], preferred_element_type=F32
+        ).astype(BF16)
+
+    @pl.when(step == pl.num_programs(0) - 1)
+    def _():
+        wide[...] = jnp.zeros_like(wide)
+        wide[:, 0:head_count] = wdt_ref[...]
+        raw = jnp.dot(table_ref[...], wide[...], preferred_element_type=F32)
+        high = raw.astype(BF16).astype(F32)
+        middle = (raw - high).astype(BF16).astype(F32)
+        low = raw - high - middle
+        tdt_ref[...] = (
+            high + pltpu.roll(middle, head_count, 1) + pltpu.roll(low, 2 * head_count, 1)
+        ).astype(BF16)
+
+
 def local_kernel(
     counts,
-    meta_ref,
+    lengths_ref,
+    ids_ref,
+    halo_ref,
+    masks_ref,
     tin_ref,
     tgate_ref,
     tdt_ref,
@@ -34,7 +68,11 @@
     ef_ref,
     state_ref,
     log_ref,
+    rowbuf,
     pbuf,
+    partbuf,
+    usebuf,
+    wide,
     scaled,
     run,
     cum,
@@ -42,34 +80,52 @@
     stretch_count, head_count, head_size, state_width, pieces = counts
     inner = head_count * head_size
     place = lax.rem(pl.program_id(0), stretch_count)
+    user = pl.program_id(0) // stretch_count
+    events = stretch_count * STRETCH
 
     @pl.when(place == 0)
     def _():
         run[...] = jnp.zeros_like(run)
         cum[...] = jnp.zeros_like(cum)
-
-    meta = jnp.transpose(meta_ref[0])
-    ids = meta[: HALO + STRETCH, 0:1].astype(jnp.int32)
-    usable = meta[:STRETCH, 1:2]
-    items = tin_ref.shape[0]
-    hot = (ids == lax.broadcasted_iota(jnp.int32, (HALO + STRETCH, items), 1)).astype(F32).astype(BF16)
-    pbuf[...] = jnp.dot(hot, tin_ref[...], preferred_element_type=F32)
-    now = hot[HALO:]
-    gate_ref[...] = jnp.dot(now, tgate_ref[...], preferred_element_type=F32).astype(BF16)
-    parts = jnp.dot(now, tdt_ref[...], preferred_element_type=F32)
+        wide[...] = jnp.zeros_like(wide)
+        wide[0:1, 0:head_count] = bias_ref[...]
+        wide[1:2, 0:head_count] = rates_ref[...]
+        first = (lax.axis_index("col") * pieces + lax.axis_index("row")) * events
+        halo = jnp.where(first == 0, -1, halo_ref[0])
+        names = jnp.concatenate([halo, ids_ref[0]], axis=1).astype(F32)
+        position = first + lax.broadcasted_iota(jnp.int32, (1, events), 1)
+        kept = jnp.where(position < lengths_ref[user], masks_ref[0], 0)
+        kept = jnp.where(kept > 0, 1.0, 0.0).astype(F32)
+        flags = jnp.concatenate([jnp.zeros((1, STRETCH), F32), kept], axis=1)
+        line = lax.broadcasted_iota(jnp.int32, (8, STRETCH + events), 0)
+        meta = jnp.transpose(jnp.where(line == 0, names, jnp.where(line == 1, flags, 0.0)))
+        usebuf[...] = meta[STRETCH:, :]
+        ids = meta[STRETCH - HALO :, 0:1].astype(jnp.int32)
+        items = tin_ref.shape[0]
+        lane = lax.broadcasted_iota(jnp.int32, (HALO + events, items), 1)
+        hot = (ids == lane).astype(F32).astype(BF16)
+        rowbuf[...] = jnp.dot(hot, tin_ref[...], preferred_element_type=F32)
+        now = hot[HALO:]
+        gate_ref[...] = jnp.dot(now, tgate_ref[...], preferred_element_type=F32).astype(BF16)
+        partbuf[...] = jnp.dot(now, tdt_ref[...], preferred_element_type=F32)
+
+    base = pl.multiple_of(place * STRETCH, STRETCH)
+    pbuf[...] = rowbuf[pl.ds(base, HALO + STRETCH), :]
+    usable = usebuf[pl.ds(base, STRETCH), :][:, 1:2]
+    parts = partbuf[pl.ds(base, STRETCH), :]
     raw = (
         parts
         + pltpu.roll(parts, LANES - head_count, 1)
         + pltpu.roll(parts, LANES - 2 * head_count, 1)
     )
-    raw = raw + bias_ref[...]
+    raw = raw + wide[0:1, :]
     step = usable * (jnp.maximum(raw, 0.0) + jnp.log1p(jnp.exp(-jnp.abs(raw))))
     rows = lax.broadcasted_iota(jnp.int32, (STRETCH, STRETCH), 0)
     cols = lax.broadcasted_iota(jnp.int32, (STRETCH, STRETCH), 1)
     causal = rows >= cols
     logs = jnp.dot(
         jnp.where(causal, 1.0, 0.0).astype(F32),
-        step * rates_ref[...],
+        step * wide[1:2, :],
         precision=lax.Precision.HIGHEST,
         preferred_element_type=F32,
     )
@@ -294,41 +350,13 @@
     head_size = inner // head_count
     state_width = (full_width - inner) // 2
     rows, cols = lax.axis_size("row"), lax.axis_size("col")
-    row_place, col_place = lax.axis_index("row"), lax.axis_index("col")
     stretch_count = events // STRETCH
     steps = users * stretch_count
     width = inner // rows
 
-    item_rows = item_ids[:, 0, :]
     order = [r * cols + c for c in range(cols) for r in range(rows)]
     route = list(zip(order[:-1], order[1:]))
-    halo = lax.ppermute(item_rows[:, events - HALO :] + 1, ("row", "col"), route) - 1
-    first_event = (col_place * rows + row_place) * events
-    position = first_event + lax.broadcasted_iota(jnp.int32, (users, events), 1)
-    usable = jnp.logical_and(position < lengths[:, None], pad_masks[:, 0, :] > 0)
-    joined = jnp.concatenate([halo, item_rows], axis=1).astype(F32)
-    padded = 2 * STRETCH
-    windows = jnp.stack(
-        [joined[:, c * STRETCH : c * STRETCH + HALO + STRETCH] for c in range(stretch_count)], axis=1
-    )
-    windows = jnp.pad(windows, ((0, 0), (0, 0), (0, padded - HALO - STRETCH)))
-    flags = jnp.pad(
-        usable.astype(F32).reshape(users, stretch_count, STRETCH),
-        ((0, 0), (0, 0), (0, padded - STRETCH)),
-    )
-    meta = jnp.pad(jnp.stack([windows, flags], axis=2), ((0, 0), (0, 0), (0, 6), (0, 0)))
-    meta = meta.reshape(steps, 8, padded)
-
-    table_in = jnp.dot(item_table, w_in, preferred_element_type=F32).astype(BF16)
-    table_gate = jnp.dot(item_table, w_gate, preferred_element_type=F32).astype(BF16)
-    raw = jnp.dot(item_table, w_dt, preferred_element_type=F32)
-    high = lax.reduce_precision(raw, 8, 7)
-    middle = lax.reduce_precision(raw - high, 8, 7)
-    low = raw - high - middle
-    table_dt = jnp.concatenate([high, middle, low], axis=1).astype(BF16)
-    table_dt = jnp.pad(table_dt, ((0, 0), (0, LANES - 3 * head_count)))
-    bias = jnp.pad(dt_bias[None], ((0, 0), (0, LANES - head_count)))
-    rates = jnp.pad(decay_rates[None], ((0, 0), (0, LANES - head_count)))
+    halo = lax.ppermute(item_ids[:, :, events - STRETCH :], ("row", "col"), route)
 
     def whole(shape):
         return pl.BlockSpec(shape, lambda s: (0,) * len(shape))
@@ -337,23 +365,60 @@
         return pl.BlockSpec((STRETCH, columns), lambda s: (s, 0))
 
     total_rows = users * events
+    block = 2 * LANES
+    in_blocks, gate_blocks = full_width // block, inner // block
+    table_in, table_gate, table_dt = pl.pallas_call(
+        functools.partial(project_kernel, (in_blocks, gate_blocks, head_count)),
+        grid=(max(in_blocks, gate_blocks),),
+        in_specs=[
+            whole((items, model)),
+            pl.BlockSpec((model, block), lambda s: (0, jnp.minimum(s, in_blocks - 1))),
+            pl.BlockSpec((model, block), lambda s: (0, jnp.minimum(s, gate_blocks - 1))),
+            whole(w_dt.shape),
+        ],
+        out_specs=[
+            pl.BlockSpec((items, block), lambda s: (0, jnp.minimum(s, in_blocks - 1))),
+            pl.BlockSpec((items, block), lambda s: (0, jnp.minimum(s, gate_blocks - 1))),
+            whole((items, LANES)),
+        ],
+        out_shape=[
+            jax.ShapeDtypeStruct((items, full_width), BF16),
+            jax.ShapeDtypeStruct((items, inner), BF16),
+            jax.ShapeDtypeStruct((items, LANES), BF16),
+        ],
+        scratch_shapes=[pltpu.VMEM((model, LANES), BF16)],
+        compiler_params=pltpu.CompilerParams(dimension_semantics=("arbitrary",)),
+        cost_estimate=pl.CostEstimate(
+            flops=2 * items * model * (full_width + inner),
+            bytes_accessed=4 * model * (full_width + inner),
+            transcendentals=0,
+        ),
+        name="table_part",
+    )(item_table, w_in, w_gate, w_dt)
+
+    def by_user(columns):
+        return pl.BlockSpec((1, 1, columns), lambda s: (s // stretch_count, 0, 0))
+
     y, gate, outward, ef, state, logs = pl.pallas_call(
         functools.partial(
             local_kernel, (stretch_count, head_count, head_size, state_width, rows)
         ),
         grid=(steps,),
         in_specs=[
-            pl.BlockSpec((1, 8, padded), lambda s: (s, 0, 0)),
+            pl.BlockSpec(memory_space=pltpu.SMEM),
+            by_user(events),
+            by_user(STRETCH),
+            by_user(events),
             whole((items, full_width)),
             whole((items, inner)),
             whole((items, LANES)),
             whole(conv_taps.shape),
-            whole((1, LANES)),
-            whole((1, LANES)),
+            whole((1, head_count)),
+            whole((1, head_count)),
         ],
         out_specs=[
             by_rows(inner),
-            by_rows(inner),
+            pl.BlockSpec((events, inner), lambda s: (s // stretch_count, 0)),
             by_rows(state_width),
             by_rows(LANES),
             pl.BlockSpec((rows, 1, state_width, width), lambda s: (0, s // stretch_count, 0, 0)),
@@ -368,14 +433,29 @@
             jax.ShapeDtypeStruct((rows, users, 8, width), F32),
         ],
         scratch_shapes=[
+            pltpu.VMEM((HALO + events, full_width), F32),
             pltpu.VMEM((HALO + STRETCH, full_width), F32),
+            pltpu.VMEM((events, LANES), F32),
+            pltpu.VMEM((events, 8), F32),
+            pltpu.VMEM((8, LANES), F32),
             pltpu.VMEM((STRETCH, inner), BF16),
             pltpu.VMEM((state_width, inner), F32),
             pltpu.VMEM((8, LANES), F32),
         ],
         compiler_params=pltpu.CompilerParams(dimension_semantics=("arbitrary",)),
         name="local_part",
-    )(meta, table_in, table_gate, table_dt, conv_taps, bias, rates)
+    )(
+        lengths,
+        item_ids,
+        halo,
+        pad_masks,
+        table_in,
+        table_gate,
+        table_dt,
+        conv_taps,
+        dt_bias[None],
+        decay_rates[None],
+    )
 
     vmem = pl.BlockSpec(memory_space=pltpu.VMEM)
     dma = pltpu.SemaphoreType.DMA
@@ -405,21 +485,26 @@
         name="state_chain",
     )(state, logs)
 
+    tall = 2 * STRETCH if events % (2 * STRETCH) == 0 else STRETCH
+
+    def tall_rows(columns):
+        return pl.BlockSpec((tall, columns), lambda s: (s, 0))
+
     result = pl.pallas_call(
         functools.partial(finish_kernel, head_count),
-        grid=(steps,),
+        grid=(total_rows // tall,),
         in_specs=[
-            by_rows(inner),
-            by_rows(inner),
-            by_rows(state_width),
-            by_rows(LANES),
-            pl.BlockSpec((rows, 1, state_width, width), lambda s: (0, s // stretch_count, 0, 0)),
+            tall_rows(inner),
+            tall_rows(inner),
+            tall_rows(state_width),
+            tall_rows(LANES),
+            pl.BlockSpec((rows, 1, state_width, width), lambda s: (0, s // (events // tall), 0, 0)),
             whole((1, inner)),
             whole(w_out.shape),
         ],
-        out_specs=by_rows(w_out.shape[1]),
+        out_specs=tall_rows(w_out.shape[1]),
         out_shape=jax.ShapeDtypeStruct((total_rows, w_out.shape[1]), BF16),
-        scratch_shapes=[pltpu.VMEM((STRETCH, inner), F32)],
+        scratch_shapes=[pltpu.VMEM((tall, inner), F32)],
         compiler_params=pltpu.CompilerParams(dimension_semantics=("arbitrary",)),
         name="finish_part",
     )(y, gate, outward, ef, entering, norm_gain[None], w_out)

time: 74.5 us -> 71.2 us (0.956)
  Pallas kernels: 55.9 us -> 64.6 us
  matrix products: 8.44 us -> 0 us
  local copies, waits for them, and re-layouts: 4.63 us -> 2.8 us
  other arithmetic: 1.65 us -> 0 us
    dot_general x3 -> x0, matrix products: 8.44 us -> none  [the longest x1 4.25 us: per_device(): jnp.dot(item_table, w_gate, preferred_element_type=F32).astype(BF16)]
    pallas_call x1 -> x2, Pallas kernels: 10.7 us -> 18 us  [the longest x1 10.1 us: per_device(): pl.pallas_call(functools.partial(finish_kernel, head_count), grid=(total_...]
    pad x4 -> x0, local copies, waits for them, and re-layouts: 3.64 us -> none  [the longest x1 1.19 us: per_device(): bias = jnp.pad(dt_bias[None], ((0, 0), (0, LANES - head_count)))]
    pallas_call x1, Pallas kernels: 18.8 us -> 20.2 us  [per_device(): pl.pallas_call(functools.partial(local_kernel, (stretch_count, head_count...]
    unnamed x6 -> x3, local copies, waits for them, and re-layouts: 0.86 us -> 2.12 us
  transfers between devices with their start and end apart: 1 -> 1, of which waited for: 0 -> 0; matrix products, arithmetic and copies ran while one was open for 18% -> 2% of each run, Pallas kernels for 0% -> 11%
where the time goes in v2:
time: 71.2 us; the launch traced here: 70.8 us
  Pallas kernels  64.6 us (91%)
  starting transfers between devices  3.39 us (5%)
  local copies, waits for them, and re-layouts  2.8 us (4%)
    pallas_call x1, Pallas kernels, per_device(): pl.pallas_call(functools.partial(chain_kernel, rows, cols), in_specs=[vme...  26.4 us
    pallas_call x1, Pallas kernels, per_device(): pl.pallas_call(functools.partial(local_kernel, (stretch_count, head_count...  20.2 us
    pallas_call x1, Pallas kernels, per_device(): pl.pallas_call(functools.partial(finish_kernel, head_count), grid=(total_...  10.1 us
    pallas_call x1, Pallas kernels, per_device(): pl.pallas_call(functools.partial(project_kernel, (in_blocks, gate_blocks,...  7.9 us
    ppermute x1, starting transfers between devices, per_device(): lax.ppermute(item_ids[:, :, events - STRETCH:], ('row', 'col'), route)  3.39 us
    unnamed x3, local copies, waits for them, and re-layouts  2.12 us
  transfers between devices with their start and end apart: 1, of which 0 were waited for; matrix products, arithmetic and copies ran while one was open for 2% of the time, Pallas kernels for 11%

profile of v2, /device:TPU:24, one launch (start us, length us, event | category | flops | bytes accessed | tf_op | source)
XLA Modules:
  0.0 70.8 jit_solution(10227563154174877723)
XLA Ops:
  0.0 0.7 slice.3
  0.7 3.4 %collective-permute-start = (s32[2,1,128]{2,1,0:T(1,128)S(1)}, s32[2,1,128]{2,1,0:T(1,128)S(1)}, u32[]{:S(2)}, u32[]{:S(2)}) collective-permute-start(s32[2,1,128]{2,1,0:T(1,128)S(1)} %slice.3), channel_id=1, source_target_pairs={{0,8},{8,16},{16,24},{24,2},{2,10},{10,18},{18,26},{26,4},{4,12},{... | collective-permute-start | bytes 3080 | tf_op jit(solution)/shard_map/ppermute | solution.py:359
  4.1 1.5 %copy.13.wdt_ref = bf16[1024,8]{1,0:T(8,128)(2,1)} copy(bf16[1024,8]{0,1:T(8,128)(2,1)} %param.18) | data formatting | bytes 32768 | tf_op args[6]
  5.6 7.9 %table_part.1 = (bf16[512,1280]{1,0:T(8,128)(2,1)}, bf16[512,1024]{1,0:T(8,128)(2,1)}, bf16[512,128]{1,0:T(8,128)(2,1)}) custom-call(bf16[512,1024]{1,0:T(8,128)(2,1)} %table_ref.1, bf16[1024,1280]{1,0:T(8,128)(2,1)} %win_ref.1, bf16[1024,1024]{1,0:T(8,128)(2,1)} %wgate_ref.1, bf16[1024,8]{1,0:T(8,128)(2,1)} %copy.13.wdt_ref), custom_call_target="tpu_custom_call" | custom-call | flops 2415919104 | bytes 9437184 | tf_op jit(solution)/shard_map/table_part/pallas_call | solution.py:370
  13.5 0.0 collective-permute-done.halo_ref
  13.5 0.0 copy-start
  13.5 0.6 copy-done
  14.1 20.2 %local_part.1 = (f32[1024,1024]{1,0:T(8,128)}, bf16[1024,1024]{1,0:T(8,128)(2,1)}, bf16[1024,128]{1,0:T(8,128)(2,1)}, f32[1024,128]{1,0:T(8,128)}, bf16[4,2,128,...) custom-call(s32[2]{0:T(128)} %lengths_ref.1, s32[2,1,512]{2,1,0:T(1,128)} %ids_ref.1, s32[2,1,128]{2,1,0:T(1,128)} %copy-done, ...), custom_call_target="tpu_custom_call" | custom-call | tf_op jit(solution)/shard_map/local_part/pallas_call | solution.py:402
  34.3 26.4 %state_chain.1.enter_ref = bf16[4,2,128,256]{3,2,1,0:T(8,128)(2,1)} custom-call(bf16[4,2,128,256]{3,2,1,0:T(8,128)(2,1)} %get-tuple-element.21.state_ref, f32[4,2,8,256]{3,2,1,0:T(8,128)} %get-tuple-element.22.log_ref), custom_call_target="tpu_custom_call" | custom-call | tf_op jit(solution)/shard_map/state_chain/pallas_call | solution.py:462
  60.7 10.1 %finish_part.1 = bf16[1024,1024]{1,0:T(8,128)(2,1)} custom-call(f32[1024,1024]{1,0:T(8,128)} %get-tuple-element.17.y_ref, bf16[1024,1024]{1,0:T(8,128)(2,1)} %get-tuple-element.18.gate_ref, bf16[1024,128]{1,0:T(8,128)(2,1)} %get-tuple-element.19.outward_ref, f32[1024,128]{1,0:T(8,128)} %get-tuple-element.20.ef_ref, ...), custom_call_target="tpu_custom_call" | custom-call | tf_op jit(solution)/shard_map/finish_part/pallas_call | solution.py:493
Async XLA Ops:
  0.7 12.9 %collective-permute-start = (s32[2,1,128]{2,1,0:T(1,128)S(1)}, s32[2,1,128]{2,1,0:T(1,128)S(1)}, u32[]{:S(2)}, u32[]{:S(2)}) collective-permute-start(s32[2,1,128]{2,1,0:T(1,128)S(1)} %slice.3), channel_id=1, source_target_pairs={{0,8},{8,16},{16,24},{24,2},{2,10},{10,18},{18,26},{26,4},{4,12},{... | collective-permute-start | bytes 3080 | tf_op jit(solution)/shard_map/ppermute | solution.py:359
  13.5 0.6 copy-start

commit v3 on v2

--- a/solution.py
+++ b/solution.py
@@ -20,8 +20,59 @@
 
 
 def project_kernel(
-    counts, table_ref, win_ref, wgate_ref, wdt_ref, tin_ref, tgate_ref, tdt_ref, wide
+    counts,
+    mesh_sizes,
+    ids_ref,
+    table_ref,
+    win_ref,
+    wgate_ref,
+    wdt_ref,
+    tin_ref,
+    tgate_ref,
+    tdt_ref,
+    halo_ref,
+    wide,
+    landed,
+    send_sem,
+    recv_sem,
 ):
+    rows, cols = mesh_sizes
+    r, c = lax.axis_index("row"), lax.axis_index("col")
+    place = c * rows + r
+    later = lax.rem(place + 1, rows * cols)
+    earlier = lax.rem(place + rows * cols - 1, rows * cols)
+    after = {"row": lax.rem(later, rows), "col": later // rows}
+    ahead = {"row": lax.rem(earlier, rows), "col": earlier // rows}
+    has_after, has_before = place < rows * cols - 1, place > 0
+    barrier = pltpu.get_barrier_semaphore()
+    events = ids_ref.shape[2]
+    copy = pltpu.make_async_remote_copy(
+        src_ref=ids_ref.at[:, :, pl.ds(events - STRETCH, STRETCH)],
+        dst_ref=landed,
+        send_sem=send_sem,
+        recv_sem=recv_sem,
+        device_id=after,
+        device_id_type=MESH,
+    )
+    begin = pl.program_id(0) == 0
+
+    @pl.when(jnp.logical_and(begin, has_before))
+    def _():
+        pl.semaphore_signal(barrier, inc=1, device_id=ahead, device_id_type=MESH)
+
+    @pl.when(jnp.logical_and(begin, has_after))
+    def _():
+        pl.semaphore_signal(barrier, inc=1, device_id=after, device_id_type=MESH)
+
+    @pl.when(pl.program_id(0) == 1)
+    def _():
+        peers = jnp.where(has_before, 1, 0) + jnp.where(has_after, 1, 0)
+        pl.semaphore_wait(barrier, peers)
+
+        @pl.when(has_after)
+        def _():
+            copy.start()
+
     in_blocks, gate_blocks, head_count = counts
     step = pl.program_id(0)
 
@@ -40,14 +91,29 @@
     @pl.when(step == pl.num_programs(0) - 1)
     def _():
         wide[...] = jnp.zeros_like(wide)
-        wide[:, 0:head_count] = wdt_ref[...]
-        raw = jnp.dot(table_ref[...], wide[...], preferred_element_type=F32)
+        wide[0:head_count, :] = wdt_ref[...]
+        raw = lax.dot_general(
+            table_ref[...], wide[...], (((1,), (1,)), ((), ())), preferred_element_type=F32
+        )
         high = raw.astype(BF16).astype(F32)
         middle = (raw - high).astype(BF16).astype(F32)
         low = raw - high - middle
         tdt_ref[...] = (
             high + pltpu.roll(middle, head_count, 1) + pltpu.roll(low, 2 * head_count, 1)
         ).astype(BF16)
+
+        @pl.when(has_after)
+        def _():
+            copy.wait_send()
+
+        @pl.when(has_before)
+        def _():
+            copy.wait_recv()
+            halo_ref[...] = landed[...]
+
+        @pl.when(place == 0)
+        def _():
+            halo_ref[...] = jnp.full(halo_ref.shape, -1, jnp.int32)
 
 
 def local_kernel(
@@ -154,7 +220,7 @@
         gap = jnp.minimum(logs_t[h : h + 1, :] - logs[:, h : h + 1], 0.0)
         weights = (jnp.exp(gap) * (scores * step_t[h : h + 1, :])).astype(BF16)
         near = jnp.dot(weights, signal[:, span], preferred_element_type=F32)
-        y_ref[:, span] = near + held[:, span] * fade[:, h : h + 1]
+        y_ref[:, span] = (near + held[:, span] * fade[:, h : h + 1]).astype(BF16)
         scaled[:, span] = (signal[:, span].astype(F32) * tail[:, h : h + 1]).astype(BF16)
     added = lax.dot_general(
         inward, scaled[...], (((0,), (0,)), ((), ())), preferred_element_type=F32
@@ -222,29 +288,41 @@
     peers = rows - 1 + jnp.where(c > 0, 1, 0) + jnp.where(c < cols - 1, 1, 0)
     pl.semaphore_wait(barrier, peers)
 
-    first = []
-    for d in range(1, rows):
-        q = lax.rem(r + d, rows)
-        for source, target, send, recv in (
-            (log_ref, lin, sl, rl),
-            (state_ref, rin, s1, r1),
-        ):
-            copy = pltpu.make_async_remote_copy(
-                src_ref=source.at[q],
-                dst_ref=target.at[r],
-                send_sem=send.at[d],
-                recv_sem=recv.at[d],
-                device_id={"row": q},
-                device_id_type=MESH,
-            )
-            copy.start()
-            first.append(copy)
+    first = [[] for _ in range(users)]
+    for u in range(users):
+        for d in range(1, rows):
+            q = lax.rem(r + d, rows)
+            for source, target, send, recv in (
+                (log_ref, lin, sl, rl),
+                (state_ref, rin, s1, r1),
+            ):
+                copy = pltpu.make_async_remote_copy(
+                    src_ref=source.at[q, u],
+                    dst_ref=target.at[r, u],
+                    send_sem=send.at[d, u],
+                    recv_sem=recv.at[d, u],
+                    device_id={"row": q},
+                    device_id_type=MESH,
+                )
+                copy.start()
+                first[u].append(copy)
     rin[r] = state_ref[r]
     lin[r] = log_ref[r]
-    for copy in first:
-        copy.wait()
+    onward = [
+        pltpu.make_async_remote_copy(
+            src_ref=psend.at[u],
+            dst_ref=pin.at[u],
+            send_sem=s2.at[u],
+            recv_sem=r2.at[u],
+            device_id={"col": lax.rem(c + 1, cols)},
+            device_id_type=MESH,
+        )
+        for u in range(users)
+    ]
 
     for u in range(users):
+        for copy in first[u]:
+            copy.wait_recv()
         carried = jnp.zeros(pin.shape[1:], F32)
         fade = jnp.ones((1, pin.shape[2]), F32)
         for m in range(rows):
@@ -255,32 +333,28 @@
             fade = fade * here
         before[rows, u] = carried
         fades[rows, u] = jnp.broadcast_to(fade, fades.shape[2:])
+        if cols > 1:
+
+            @pl.when(c == 0)
+            def _(u=u, carried=carried):
+                psend[u] = carried.astype(BF16)
+                onward[u].start()
 
     @pl.when(c == 0)
     def _():
         pin[...] = jnp.zeros_like(pin)
 
-    second = []
     third = []
     for u in range(users):
-        copy = pltpu.make_async_remote_copy(
-            src_ref=psend.at[u],
-            dst_ref=pin.at[u],
-            send_sem=s2.at[u],
-            recv_sem=r2.at[u],
-            device_id={"col": lax.rem(c + 1, cols)},
-            device_id_type=MESH,
-        )
-        second.append(copy)
 
         @pl.when(c > 0)
-        def _(copy=copy):
-            copy.wait_recv()
-
-        @pl.when(c < cols - 1)
-        def _(copy=copy, u=u):
+        def _(u=u):
+            onward[u].wait_recv()
+
+        @pl.when(jnp.logical_and(c > 0, c < cols - 1))
+        def _(u=u):
             psend[u] = (fades[rows, u, 0:1, :] * pin[u].astype(F32) + before[rows, u]).astype(BF16)
-            copy.start()
+            onward[u].start()
 
         for d in range(1, rows):
             q = lax.rem(r + d, rows)
@@ -298,10 +372,13 @@
         enter_ref[r, u] = (fades[r, u, 0:1, :] * pin[u].astype(F32) + before[r, u]).astype(BF16)
     for copy in third:
         copy.wait()
+    for group in first:
+        for copy in group:
+            copy.wait_send()
 
     @pl.when(c < cols - 1)
     def _():
-        for copy in second:
+        for copy in onward:
             copy.wait_send()
 
 
@@ -317,7 +394,7 @@
         for j in range(width // head_size):
             h = q * (width // head_size) + j
             span = slice(h * head_size, (h + 1) * head_size)
-            both = y_ref[:, span] + far[:, j * head_size : (j + 1) * head_size] * ef_ref[:, h : h + 1]
+            both = y_ref[:, span].astype(F32) + far[:, j * head_size : (j + 1) * head_size] * ef_ref[:, h : h + 1]
             value = both * silu(gate_ref[:, span].astype(F32))
             mix[:, span] = value
             squares = value * value if squares is None else squares + value * value
@@ -354,10 +431,6 @@
     steps = users * stretch_count
     width = inner // rows
 
-    order = [r * cols + c for c in range(cols) for r in range(rows)]
-    route = list(zip(order[:-1], order[1:]))
-    halo = lax.ppermute(item_ids[:, :, events - STRETCH :], ("row", "col"), route)
-
     def whole(shape):
         return pl.BlockSpec(shape, lambda s: (0,) * len(shape))
 
@@ -367,34 +440,44 @@
     total_rows = users * events
     block = 2 * LANES
     in_blocks, gate_blocks = full_width // block, inner // block
-    table_in, table_gate, table_dt = pl.pallas_call(
-        functools.partial(project_kernel, (in_blocks, gate_blocks, head_count)),
+    table_in, table_gate, table_dt, halo = pl.pallas_call(
+        functools.partial(project_kernel, (in_blocks, gate_blocks, head_count), (rows, cols)),
         grid=(max(in_blocks, gate_blocks),),
         in_specs=[
+            whole(item_ids.shape),
             whole((items, model)),
             pl.BlockSpec((model, block), lambda s: (0, jnp.minimum(s, in_blocks - 1))),
             pl.BlockSpec((model, block), lambda s: (0, jnp.minimum(s, gate_blocks - 1))),
-            whole(w_dt.shape),
+            whole(w_dt.shape[::-1]),
         ],
         out_specs=[
             pl.BlockSpec((items, block), lambda s: (0, jnp.minimum(s, in_blocks - 1))),
             pl.BlockSpec((items, block), lambda s: (0, jnp.minimum(s, gate_blocks - 1))),
             whole((items, LANES)),
+            whole((users, 1, STRETCH)),
         ],
         out_shape=[
             jax.ShapeDtypeStruct((items, full_width), BF16),
             jax.ShapeDtypeStruct((items, inner), BF16),
             jax.ShapeDtypeStruct((items, LANES), BF16),
-        ],
-        scratch_shapes=[pltpu.VMEM((model, LANES), BF16)],
-        compiler_params=pltpu.CompilerParams(dimension_semantics=("arbitrary",)),
+            jax.ShapeDtypeStruct((users, 1, STRETCH), jnp.int32),
+        ],
+        scratch_shapes=[
+            pltpu.VMEM((LANES, model), BF16),
+            pltpu.VMEM((users, 1, STRETCH), jnp.int32),
+            pltpu.SemaphoreType.DMA,
+            pltpu.SemaphoreType.DMA,
+        ],
+        compiler_params=pltpu.CompilerParams(
+            dimension_semantics=("arbitrary",), collective_id=1, has_side_effects=True
+        ),
         cost_estimate=pl.CostEstimate(
             flops=2 * items * model * (full_width + inner),
             bytes_accessed=4 * model * (full_width + inner),
             transcendentals=0,
         ),
         name="table_part",
-    )(item_table, w_in, w_gate, w_dt)
+    )(item_ids, item_table, w_in, w_gate, w_dt.T)
 
     def by_user(columns):
         return pl.BlockSpec((1, 1, columns), lambda s: (s // stretch_count, 0, 0))
@@ -425,7 +508,7 @@
             pl.BlockSpec((rows, 1, 8, width), lambda s: (0, s // stretch_count, 0, 0)),
         ],
         out_shape=[
-            jax.ShapeDtypeStruct((total_rows, inner), F32),
+            jax.ShapeDtypeStruct((total_rows, inner), BF16),
             jax.ShapeDtypeStruct((total_rows, inner), BF16),
             jax.ShapeDtypeStruct((total_rows, state_width), BF16),
             jax.ShapeDtypeStruct((total_rows, LANES), F32),
@@ -472,10 +555,10 @@
             pltpu.VMEM(state.shape[1:], BF16),
             pltpu.VMEM(state.shape[1:], BF16),
             pltpu.VMEM(state.shape, BF16),
-            dma((rows,)),
-            dma((rows,)),
-            dma((rows,)),
-            dma((rows,)),
+            dma((rows, users)),
+            dma((rows, users)),
+            dma((rows, users)),
+            dma((rows, users)),
             dma((users,)),
             dma((users,)),
             dma((rows, users)),

time: 71.2 us -> 63.4 us (0.89)
  starting transfers between devices: 3.39 us -> 0 us
  local copies, waits for them, and re-layouts: 2.8 us -> 0 us
  Pallas kernels: 64.6 us -> 63.2 us
    ppermute x1 -> x0, starting transfers between devices: 3.39 us -> none  [per_device(): lax.ppermute(item_ids[:, :, events - STRETCH:], ('row', 'col'), route)]
    pallas_call x1, Pallas kernels: 26.4 us -> 24 us  [per_device(): pl.pallas_call(functools.partial(chain_kernel, rows, cols), in_specs=[vme...]
    unnamed x3 -> x0, local copies, waits for them, and re-layouts: 2.12 us -> none
    pallas_call x1, Pallas kernels: 7.9 us -> 9.1 us  [per_device(): pl.pallas_call(functools.partial(project_kernel, (in_blocks, gate_blocks,...]
  transfers between devices with their start and end apart: 1 -> 0, of which waited for: 0 -> 0; matrix products, arithmetic and copies ran while one was open for 2% -> 0% of each run, Pallas kernels for 11% -> 0%
where the time goes in v3:
time: 63.4 us; the launch traced here: 63.2 us
  Pallas kernels  63.2 us (100%)
    pallas_call x1, Pallas kernels, per_device(): pl.pallas_call(functools.partial(chain_kernel, rows, cols), in_specs=[vme...  24 us
    pallas_call x1, Pallas kernels, per_device(): pl.pallas_call(functools.partial(local_kernel, (stretch_count, head_count...  20.2 us
    pallas_call x1, Pallas kernels, per_device(): pl.pallas_call(functools.partial(finish_kernel, head_count), grid=(total_...  9.91 us
    pallas_call x1, Pallas kernels, per_device(): pl.pallas_call(functools.partial(project_kernel, (in_blocks, gate_blocks,...  9.1 us

profile of v3, /device:TPU:24, one launch (start us, length us, event | category | flops | bytes accessed | tf_op | source)
XLA Modules:
  0.0 63.2 jit_solution(11316252108346213910)
XLA Ops:
  0.0 9.1 %table_part.1 = (bf16[512,1280]{1,0:T(8,128)(2,1)}, bf16[512,1024]{1,0:T(8,128)(2,1)}, bf16[512,128]{1,0:T(8,128)(2,1)}, s32[2,1,128]{2,1,0:T(1,128)}) custom-call(s32[2,1,512]{2,1,0:T(1,128)} %ids_ref.3, bf16[512,1024]{1,0:T(8,128)(2,1)} %table_ref.1, bf16[1024,1280]{1,0:T(8,128)(2,1)} %win_ref.1, bf16[1024,1024]{1,0:T(8,128)(2,1)} %wgate_ref.1, ...), custom_call_target="tpu_custom_call" | custom-call | flops 2415919104 | bytes 9437184 | tf_op jit(solution)/shard_map/table_part/pallas_call | solution.py:443
  9.1 20.2 %local_part.1 = (bf16[1024,1024]{1,0:T(8,128)(2,1)}, bf16[1024,1024]{1,0:T(8,128)(2,1)}, bf16[1024,128]{1,0:T(8,128)(2,1)}, f32[1024,128]{1,0:T(8,128)}, bf16[4,...) custom-call(s32[2]{0:T(128)} %lengths_ref.1, s32[2,1,512]{2,1,0:T(1,128)} %ids_ref.3, ...), custom_call_target="tpu_custom_call" | custom-call | tf_op jit(solution)/shard_map/local_part/pallas_call | solution.py:485
  29.3 24.0 %state_chain.1.enter_ref = bf16[4,2,128,256]{3,2,1,0:T(8,128)(2,1)} custom-call(bf16[4,2,128,256]{3,2,1,0:T(8,128)(2,1)} %get-tuple-element.23.state_ref, f32[4,2,8,256]{3,2,1,0:T(8,128)} %get-tuple-element.24.log_ref), custom_call_target="tpu_custom_call" | custom-call | tf_op jit(solution)/shard_map/state_chain/pallas_call | solution.py:545
  53.3 9.9 %finish_part.1 = bf16[1024,1024]{1,0:T(8,128)(2,1)} custom-call(bf16[1024,1024]{1,0:T(8,128)(2,1)} %get-tuple-element.19.y_ref, bf16[1024,1024]{1,0:T(8,128)(2,1)} %get-tuple-element.20.gate_ref, bf16[1024,128]{1,0:T(8,128)(2,1)} %get-tuple-element.21.outward_ref, f32[1024,128]{1,0:T(8,128)} %get-tuple-element.22.ef_ref, ...), custom_call_target="tpu_custom_call" | custom-call | tf_op jit(solution)/shard_map/finish_part/pallas_call | solution.py:576

commit v4 on v3

--- a/solution.py
+++ b/solution.py
@@ -135,7 +135,6 @@
     state_ref,
     log_ref,
     rowbuf,
-    pbuf,
     partbuf,
     usebuf,
     wide,
@@ -176,7 +175,6 @@
         partbuf[...] = jnp.dot(now, tdt_ref[...], preferred_element_type=F32)
 
     base = pl.multiple_of(place * STRETCH, STRETCH)
-    pbuf[...] = rowbuf[pl.ds(base, HALO + STRETCH), :]
     usable = usebuf[pl.ds(base, STRETCH), :][:, 1:2]
     parts = partbuf[pl.ds(base, STRETCH), :]
     raw = (
@@ -199,11 +197,11 @@
     logs_t = jnp.transpose(logs)
     step_t = jnp.transpose(step)
     kernel = taps_ref.shape[0]
-    conv = None
-    for k in range(kernel):
-        start = HALO - (kernel - 1) + k
-        term = pbuf[start : start + STRETCH, :] * taps_ref[k : k + 1, :]
-        conv = term if conv is None else conv + term
+    window = rowbuf[pl.ds(base, HALO + STRETCH), :]
+    conv = window * taps_ref[0:1, :]
+    for k in range(1, kernel):
+        conv = pltpu.roll(conv, 1, 0) + window * taps_ref[k : k + 1, :]
+    conv = conv[HALO:, :]
     signal = silu(conv[:, :inner]).astype(BF16)
     inward = conv[:, inner : inner + state_width].astype(BF16)
     outward = conv[:, inner + state_width :].astype(BF16)
@@ -517,7 +515,6 @@
         ],
         scratch_shapes=[
             pltpu.VMEM((HALO + events, full_width), F32),
-            pltpu.VMEM((HALO + STRETCH, full_width), F32),
             pltpu.VMEM((events, LANES), F32),
             pltpu.VMEM((events, 8), F32),
             pltpu.VMEM((8, LANES), F32),

time: 63.4 us -> 61.4 us (0.968)
  Pallas kernels: 63.2 us -> 61.1 us
    pallas_call x1, Pallas kernels: 20.2 us -> 18.1 us  [per_device(): pl.pallas_call(functools.partial(local_kernel, (stretch_count, head_count...]
where the time goes in v4:
time: 61.4 us; the launch traced here: 61.1 us
  Pallas kernels  61.1 us (100%)
    pallas_call x1, Pallas kernels, per_device(): pl.pallas_call(functools.partial(chain_kernel, rows, cols), in_specs=[vme...  24 us
    pallas_call x1, Pallas kernels, per_device(): pl.pallas_call(functools.partial(local_kernel, (stretch_count, head_count...  18.1 us
    pallas_call x1, Pallas kernels, per_device(): pl.pallas_call(functools.partial(finish_kernel, head_count), grid=(total_...  9.91 us
    pallas_call x1, Pallas kernels, per_device(): pl.pallas_call(functools.partial(project_kernel, (in_blocks, gate_blocks,...  9.1 us

profile of v4, /device:TPU:24, one launch (start us, length us, event | category | flops | bytes accessed | tf_op | source)
XLA Modules:
  0.0 61.1 jit_solution(285058290990596040)
XLA Ops:
  0.0 9.1 %table_part.1 = (bf16[512,1280]{1,0:T(8,128)(2,1)}, bf16[512,1024]{1,0:T(8,128)(2,1)}, bf16[512,128]{1,0:T(8,128)(2,1)}, s32[2,1,128]{2,1,0:T(1,128)}) custom-call(s32[2,1,512]{2,1,0:T(1,128)} %ids_ref.3, bf16[512,1024]{1,0:T(8,128)(2,1)} %table_ref.1, bf16[1024,1280]{1,0:T(8,128)(2,1)} %win_ref.1, bf16[1024,1024]{1,0:T(8,128)(2,1)} %wgate_ref.1, ...), custom_call_target="tpu_custom_call" | custom-call | flops 2415919104 | bytes 9437184 | tf_op jit(solution)/shard_map/table_part/pallas_call | solution.py:441
  9.1 18.1 %local_part.1 = (bf16[1024,1024]{1,0:T(8,128)(2,1)}, bf16[1024,1024]{1,0:T(8,128)(2,1)}, bf16[1024,128]{1,0:T(8,128)(2,1)}, f32[1024,128]{1,0:T(8,128)}, bf16[4,...) custom-call(s32[2]{0:T(128)} %lengths_ref.1, s32[2,1,512]{2,1,0:T(1,128)} %ids_ref.3, ...), custom_call_target="tpu_custom_call" | custom-call | tf_op jit(solution)/shard_map/local_part/pallas_call | solution.py:483
  27.2 24.0 %state_chain.1.enter_ref = bf16[4,2,128,256]{3,2,1,0:T(8,128)(2,1)} custom-call(bf16[4,2,128,256]{3,2,1,0:T(8,128)(2,1)} %get-tuple-element.23.state_ref, f32[4,2,8,256]{3,2,1,0:T(8,128)} %get-tuple-element.24.log_ref), custom_call_target="tpu_custom_call" | custom-call | tf_op jit(solution)/shard_map/state_chain/pallas_call | solution.py:542
  51.2 9.9 %finish_part.1 = bf16[1024,1024]{1,0:T(8,128)(2,1)} custom-call(bf16[1024,1024]{1,0:T(8,128)(2,1)} %get-tuple-element.19.y_ref, bf16[1024,1024]{1,0:T(8,128)(2,1)} %get-tuple-element.20.gate_ref, bf16[1024,128]{1,0:T(8,128)(2,1)} %get-tuple-element.21.outward_ref, f32[1024,128]{1,0:T(8,128)} %get-tuple-element.22.ef_ref, ...), custom_call_target="tpu_custom_call" | custom-call | tf_op jit(solution)/shard_map/finish_part/pallas_call | solution.py:573
